TPU v7x, 32 devices: a whole 2x2x4 slice. The times are simulated.
32 devices in a mesh: fsdp: 4 (over z), ctx: 4 (over x, core), tp: 2 (over y).
Axes of the slice: x: 2, y: 2, z: 4, core: 2. Of those that a mesh axis runs over, the one named last changes fastest.
Arguments:
- layer_input: float32 [4, 4096, 512], P('fsdp', 'ctx'), may hold values from -6 to 6
- out_grad: float32 [4, 4096, 512], P('fsdp', 'ctx'), may hold values from -6 to 6
- lengths: int32 [4], P('fsdp'), may hold values from 1024 to 4096, as said below
- norm_gains: float32 [5, 512], replicated, may hold values from 0.5 to 1.5
- feed_up: bfloat16 [512, 2048], P('fsdp', 'tp'), may hold values from -0.25 to 0.25
- feed_down: bfloat16 [512, 2048], P('fsdp', 'tp'), may hold values from -0.125 to 0.125
- attend_in: bfloat16 [512, 3, 512], P('fsdp', None, 'tp'), may hold values from -0.25 to 0.25
- attend_out: bfloat16 [512, 512], P('fsdp', 'tp'), may hold values from -6 to 6
- mixer_in: bfloat16 [512, 2, 512], P('fsdp', None, 'tp'), may hold values from -0.25 to 0.25
- mixer_out: bfloat16 [512, 512], P('fsdp', 'tp'), may hold values from -0.25 to 0.25
- depth_kernel: float32 [31, 512], P(None, 'tp'), may hold values from -1.5 to 1.5
- batch_norm: float32 [2, 512], P(None, 'tp'), may hold values from 0.5 to 1.5
- final_up: bfloat16 [512, 2048], P('fsdp', 'tp'), may hold values from -0.25 to 0.25
- final_down: bfloat16 [512, 2048], P('fsdp', 'tp'), may hold values from -0.125 to 0.125
Outputs:
- layer_output: float32 [4, 4096, 512], P('fsdp', 'ctx')
- input_grad: float32 [4, 4096, 512], P('fsdp', 'ctx')
- gains_grad: float32 [5, 512], replicated
- feed_up_grad: float32 [512, 2048], P('fsdp', 'tp')
- feed_down_grad: float32 [512, 2048], P('fsdp', 'tp')
- attend_in_grad: float32 [512, 3, 512], P('fsdp', None, 'tp')
- attend_out_grad: float32 [512, 512], P('fsdp', 'tp')
- mixer_in_grad: float32 [512, 2, 512], P('fsdp', None, 'tp')
- mixer_out_grad: float32 [512, 512], P('fsdp', 'tp')
- kernel_grad: float32 [31, 512], P(None, 'tp')
- norm_grad: float32 [2, 512], P(None, 'tp')
- final_up_grad: float32 [512, 2048], P('fsdp', 'tp')
- final_down_grad: float32 [512, 2048], P('fsdp', 'tp')
Inputs may be any that keep to these rules, and one draw needn't show every extreme that they name: `lengths`: every utterance has at least a quarter of its 4096 frames, and one of them has all 4096.
All inputs are finite; a program needn't handle non-finite values.
Results may differ from a plain program's by a relative error of at most 0.038.
Values may be sent and summed in bfloat16 or wider, within the bound.
A program may use at most 384 MiB of HBM per device.

v0:
```python
import jax
import jax.numpy as jnp
from jax import lax
from jax.sharding import PartitionSpec as P

HEAD = 64
KERNEL = 31
norm_eps = 1e-05
masked_score = -1000000000.0


def with_halo(cells, sides, width):
    for axis, dim in sides:
        count = lax.axis_size(axis)
        ends = count - 1
        head = lax.slice_in_dim(cells, 0, width, axis=dim)
        tail = lax.slice_in_dim(cells, cells.shape[dim] - width, cells.shape[dim], axis=dim)
        cells = jnp.concatenate(
            [
                lax.ppermute(tail, axis, [(i, (i + 1) % count) for i in range(ends)]),
                cells,
                lax.ppermute(head, axis, [((i + 1) % count, i) for i in range(ends)]),
            ],
            axis=dim,
        )
    return cells


def layer_norm(values, gain):
    center = values - jnp.mean(values, -1, keepdims=True)
    spread = jnp.mean(center * center, -1, keepdims=True)
    return center * lax.rsqrt(spread + norm_eps) * gain


def rotary(values, position):
    half = values.shape[-1] // 2
    inverse = 10000.0 ** (-2.0 * jnp.arange(half, dtype=jnp.float32) / values.shape[-1])
    angle = position.astype(jnp.float32)[:, None] * inverse[None, :]
    cosine = jnp.cos(angle)[:, None, :]
    sine = jnp.sin(angle)[:, None, :]
    lower = values[..., :half]
    upper = values[..., half:]
    return jnp.concatenate([lower * cosine - upper * sine, lower * sine + upper * cosine], -1)


def swish(values):
    return values * jax.nn.sigmoid(values)


def tensor_total(partial_value):
    return lax.psum(partial_value.astype(jnp.bfloat16), "tp").astype(jnp.float32)


def product_rows(left, right):
    return lax.dot_general(
        left, right, (((1,), (1,)), ((), ())), preferred_element_type=jnp.float32
    )


def product_cols(left, right):
    return lax.dot_general(
        left, right, (((0,), (0,)), ((), ())), preferred_element_type=jnp.float32
    )


def feed_forward(stream, gain, weight_up, weight_down):
    normed, norm_back = jax.vjp(layer_norm, stream, gain)
    normed_low = normed.astype(jnp.bfloat16)
    hidden = jnp.dot(normed_low, weight_up, preferred_element_type=jnp.float32)
    active, active_back = jax.vjp(swish, hidden)
    active_low = active.astype(jnp.bfloat16)
    branch = tensor_total(product_rows(active_low, weight_down))
    return (branch, (norm_back, normed_low, active_back, active_low))


def feed_backward(branch_grad, saved, weight_up, weight_down):
    norm_back, normed_low, active_back, active_low = saved
    grad_low = branch_grad.astype(jnp.bfloat16)
    down_grad = product_cols(grad_low, active_low)
    hidden_grad = active_back(jnp.dot(grad_low, weight_down, preferred_element_type=jnp.float32))[
        0
    ].astype(jnp.bfloat16)
    up_grad = product_cols(normed_low, hidden_grad)
    normed_grad = tensor_total(product_rows(hidden_grad, weight_up))
    stream_grad, gain_grad = norm_back(normed_grad)
    return (stream_grad, gain_grad, up_grad, down_grad)


def split_joined(joined, heads):
    width = heads * HEAD
    keys = joined[:, :width].reshape(joined.shape[0], heads, HEAD)
    values = joined[:, width:].reshape(joined.shape[0], heads, HEAD)
    return (keys, values)


def attend_scores(query, keys, length):
    scores = jnp.einsum("fhe,lhe->hfl", query, keys, preferred_element_type=jnp.float32)
    live_keys = jnp.arange(keys.shape[0]) < length
    return jnp.where(live_keys[None, None, :], scores, masked_score)


def attend_one(inputs):
    query, joined, length = inputs
    keys, values = split_joined(joined, query.shape[1])
    scores = attend_scores(query, keys, length)
    top = jnp.max(scores, -1, keepdims=True)
    raised = jnp.exp(scores - top)
    total = jnp.sum(raised, -1, keepdims=True)
    weights = (raised / total).astype(jnp.bfloat16)
    mixed = jnp.einsum("hfl,lhe->fhe", weights, values, preferred_element_type=jnp.float32)
    return (mixed.astype(jnp.bfloat16), (top + jnp.log(total))[..., 0])


def attend_back(inputs):
    query, joined, length, log_total, mixed_grad = inputs
    keys, values = split_joined(joined, query.shape[1])
    scores = attend_scores(query, keys, length)
    probs = jnp.exp(scores - log_total[..., None])
    probs_grad = jnp.einsum("fhe,lhe->hfl", mixed_grad, values, preferred_element_type=jnp.float32)
    center = jnp.sum(probs * probs_grad, -1, keepdims=True)
    score_grad = (probs * (probs_grad - center)).astype(jnp.bfloat16)
    query_grad = jnp.einsum("hfl,lhe->fhe", score_grad, keys, preferred_element_type=jnp.float32)
    keys_grad = jnp.einsum("hfl,fhe->lhe", score_grad, query, preferred_element_type=jnp.float32)
    values_grad = jnp.einsum(
        "hfl,fhe->lhe", probs.astype(jnp.bfloat16), mixed_grad, preferred_element_type=jnp.float32
    )
    frames_all = keys.shape[0]
    joined_grad = jnp.concatenate(
        [keys_grad.reshape(frames_all, -1), values_grad.reshape(frames_all, -1)], -1
    )
    return (query_grad, joined_grad)


def per_device(
    layer_input,
    out_grad,
    lengths,
    norm_gains,
    feed_up,
    feed_down,
    attend_in,
    attend_out,
    mixer_in,
    mixer_out,
    depth_kernel,
    batch_norm,
    final_up,
    final_down,
):
    batch, frames, width = layer_input.shape
    rows = batch * frames
    place = lax.axis_index("ctx") * frames + jnp.arange(frames, dtype=jnp.int32)
    live = (place[None, :] < lengths[:, None]).astype(jnp.float32)
    live_rows = live.reshape(rows, 1)
    live_cube = live[:, :, None]
    gathered = (
        lax.all_gather(feed_up, "fsdp", axis=0, tiled=True),
        lax.all_gather(feed_down, "fsdp", axis=0, tiled=True),
        lax.all_gather(attend_in, "fsdp", axis=0, tiled=True),
        lax.all_gather(attend_out, "fsdp", axis=0, tiled=True),
        lax.all_gather(mixer_in, "fsdp", axis=0, tiled=True),
        lax.all_gather(mixer_out, "fsdp", axis=0, tiled=True),
        lax.all_gather(final_up, "fsdp", axis=0, tiled=True),
        lax.all_gather(final_down, "fsdp", axis=0, tiled=True),
    )
    up_one, down_one, proj_in, proj_out, conv_in, conv_out, up_two, down_two = gathered
    stream = layer_input.reshape(rows, width)
    cotangent = out_grad.reshape(rows, width)
    branch_one, saved_one = feed_forward(stream, norm_gains[0], up_one, down_one)
    after_one = stream + 0.5 * branch_one
    normed, norm_back_two = jax.vjp(layer_norm, after_one, norm_gains[1])
    normed_two = normed.astype(jnp.bfloat16)
    projected = jnp.einsum("nd,dke->nke", normed_two, proj_in, preferred_element_type=jnp.float32)
    local_width = projected.shape[2]
    heads = local_width // HEAD
    split = projected.reshape(batch, frames, 3, heads, HEAD)

    def rotate_pair(query_raw, key_raw):
        return (rotary(query_raw, place) * HEAD ** (-0.5), rotary(key_raw, place))

    (query_rot, key_rot), rotate_back = jax.vjp(rotate_pair, split[:, :, 0], split[:, :, 1])
    query_low = query_rot.astype(jnp.bfloat16)
    joined = jnp.concatenate(
        [
            key_rot.astype(jnp.bfloat16).reshape(batch, frames, local_width),
            split[:, :, 2].astype(jnp.bfloat16).reshape(batch, frames, local_width),
        ],
        -1,
    )
    joined_all = lax.all_gather(joined, "ctx", axis=1, tiled=True)
    mixed, log_total = lax.map(attend_one, (query_low, joined_all, lengths))
    mixed_rows = mixed.reshape(rows, local_width)
    after_two = after_one + tensor_total(product_rows(mixed_rows, proj_out))
    normed, norm_back_three = jax.vjp(layer_norm, after_two, norm_gains[2])
    normed_three = normed.astype(jnp.bfloat16)
    gates = jnp.einsum("nd,dke->nke", normed_three, conv_in, preferred_element_type=jnp.float32)

    def gate_linear(values):
        return values[:, 0] * jax.nn.sigmoid(values[:, 1]) * live_rows

    gated, gate_back = jax.vjp(gate_linear, gates)
    channels = gated.shape[1]
    gated_low = gated.astype(jnp.bfloat16).reshape(batch, frames, channels)
    reach = KERNEL // 2
    padded = with_halo(gated_low, (("ctx", 1),), reach)
    filtered = jnp.zeros((batch, frames, channels), jnp.float32)
    for offset in range(KERNEL):
        filtered = filtered + depth_kernel[offset] * padded[:, offset : offset + frames].astype(
            jnp.float32
        )
    sums = lax.psum(
        (
            jnp.sum(live_cube * filtered, (0, 1)),
            jnp.sum(live_cube * filtered * filtered, (0, 1)),
            jnp.sum(live),
        ),
        ("fsdp", "ctx"),
    )
    count = sums[2]
    mean = sums[0] / count
    variance = sums[1] / count - mean * mean
    rescale = lax.rsqrt(variance + norm_eps)
    unit = (filtered - mean) * rescale
    shifted = unit * batch_norm[0] + batch_norm[1]
    active, active_back = jax.vjp(swish, shifted.reshape(rows, channels))
    active_low = active.astype(jnp.bfloat16)
    after_three = after_two + tensor_total(product_rows(active_low, conv_out))
    branch_four, saved_four = feed_forward(after_three, norm_gains[3], up_two, down_two)
    after_four = after_three + 0.5 * branch_four
    result, final_back = jax.vjp(layer_norm, after_four, norm_gains[4])
    grad_four, gain_five = final_back(cotangent)
    stream_grad, gain_four, up_two_grad, down_two_grad = feed_backward(
        0.5 * grad_four, saved_four, up_two, down_two
    )
    grad_three = grad_four + stream_grad
    branch_low = grad_three.astype(jnp.bfloat16)
    conv_out_grad = product_cols(branch_low, active_low)
    shifted_grad = active_back(jnp.dot(branch_low, conv_out, preferred_element_type=jnp.float32))[
        0
    ].reshape(batch, frames, channels)
    bias_sum, scale_sum = lax.psum(
        (jnp.sum(shifted_grad, (0, 1)), jnp.sum(shifted_grad * unit, (0, 1))), ("fsdp", "ctx")
    )
    var_grad = -0.5 * rescale * rescale * batch_norm[0] * scale_sum
    first_grad = (-rescale * batch_norm[0] * bias_sum - 2.0 * mean * var_grad) / count
    second_grad = var_grad / count
    filtered_grad = (
        rescale * batch_norm[0] * shifted_grad
        + live_cube * (first_grad + 2.0 * filtered * second_grad)
    ).astype(jnp.bfloat16)
    padded_grad = with_halo(filtered_grad, (("ctx", 1),), reach)
    filtered_wide = filtered_grad.astype(jnp.float32)
    gated_grad = jnp.zeros((batch, frames, channels), jnp.float32)
    kernel_terms = []
    for offset in range(KERNEL):
        start = 2 * reach - offset
        gated_grad = gated_grad + depth_kernel[offset] * padded_grad[
            :, start : start + frames
        ].astype(jnp.float32)
        kernel_terms.append(
            jnp.sum(filtered_wide * padded[:, offset : offset + frames].astype(jnp.float32), (0, 1))
        )
    kernel_local = jnp.stack(kernel_terms)
    gates_grad = gate_back(gated_grad.reshape(rows, channels))[0].astype(jnp.bfloat16)
    conv_in_grad = jnp.einsum(
        "nd,nke->dke", normed_three, gates_grad, preferred_element_type=jnp.float32
    )
    normed_grad = tensor_total(
        jnp.einsum("nke,dke->nd", gates_grad, conv_in, preferred_element_type=jnp.float32)
    )
    stream_grad, gain_three = norm_back_three(normed_grad)
    grad_two = grad_three + stream_grad
    branch_low = grad_two.astype(jnp.bfloat16)
    proj_out_grad = product_cols(branch_low, mixed_rows)
    mixed_grad = (
        jnp.dot(branch_low, proj_out, preferred_element_type=jnp.float32)
        .astype(jnp.bfloat16)
        .reshape(batch, frames, heads, HEAD)
    )
    query_grad, joined_grad = lax.map(
        attend_back, (query_low, joined_all, lengths, log_total, mixed_grad)
    )
    joined_local = lax.psum_scatter(
        joined_grad.astype(jnp.bfloat16), "ctx", scatter_dimension=1, tiled=True
    ).astype(jnp.float32)
    key_grad = joined_local[..., :local_width].reshape(batch, frames, heads, HEAD)
    value_grad = joined_local[..., local_width:].reshape(batch, frames, heads, HEAD)
    query_raw_grad, key_raw_grad = rotate_back((query_grad, key_grad))
    proj_grad = (
        jnp.stack([query_raw_grad, key_raw_grad, value_grad], 2)
        .reshape(rows, 3, local_width)
        .astype(jnp.bfloat16)
    )
    proj_in_grad = jnp.einsum(
        "nd,nke->dke", normed_two, proj_grad, preferred_element_type=jnp.float32
    )
    normed_grad = tensor_total(
        jnp.einsum("nke,dke->nd", proj_grad, proj_in, preferred_element_type=jnp.float32)
    )
    stream_grad, gain_two = norm_back_two(normed_grad)
    grad_one = grad_two + stream_grad
    stream_grad, gain_one, up_one_grad, down_one_grad = feed_backward(
        0.5 * grad_one, saved_one, up_one, down_one
    )
    input_grad = grad_one + stream_grad
    gain_terms = jnp.stack([gain_one, gain_two, gain_three, gain_four, gain_five])
    gain_total, kernel_total = lax.psum((gain_terms, kernel_local), ("fsdp", "ctx"))
    weight_grads = (
        up_one_grad,
        down_one_grad,
        proj_in_grad,
        proj_out_grad,
        conv_in_grad,
        conv_out_grad,
        up_two_grad,
        down_two_grad,
    )
    owned = (
        lax.psum_scatter(
            weight_grads[0].astype(jnp.bfloat16), "fsdp", scatter_dimension=0, tiled=True
        ).astype(jnp.float32),
        lax.psum_scatter(
            weight_grads[1].astype(jnp.bfloat16), "fsdp", scatter_dimension=0, tiled=True
        ).astype(jnp.float32),
        lax.psum_scatter(
            weight_grads[2].astype(jnp.bfloat16), "fsdp", scatter_dimension=0, tiled=True
        ).astype(jnp.float32),
        lax.psum_scatter(
            weight_grads[3].astype(jnp.bfloat16), "fsdp", scatter_dimension=0, tiled=True
        ).astype(jnp.float32),
        lax.psum_scatter(
            weight_grads[4].astype(jnp.bfloat16), "fsdp", scatter_dimension=0, tiled=True
        ).astype(jnp.float32),
        lax.psum_scatter(
            weight_grads[5].astype(jnp.bfloat16), "fsdp", scatter_dimension=0, tiled=True
        ).astype(jnp.float32),
        lax.psum_scatter(
            weight_grads[6].astype(jnp.bfloat16), "fsdp", scatter_dimension=0, tiled=True
        ).astype(jnp.float32),
        lax.psum_scatter(
            weight_grads[7].astype(jnp.bfloat16), "fsdp", scatter_dimension=0, tiled=True
        ).astype(jnp.float32),
    )
    owned = (
        lax.psum(owned[0].astype(jnp.bfloat16), "ctx").astype(jnp.float32),
        lax.psum(owned[1].astype(jnp.bfloat16), "ctx").astype(jnp.float32),
        lax.psum(owned[2].astype(jnp.bfloat16), "ctx").astype(jnp.float32),
        lax.psum(owned[3].astype(jnp.bfloat16), "ctx").astype(jnp.float32),
        lax.psum(owned[4].astype(jnp.bfloat16), "ctx").astype(jnp.float32),
        lax.psum(owned[5].astype(jnp.bfloat16), "ctx").astype(jnp.float32),
        lax.psum(owned[6].astype(jnp.bfloat16), "ctx").astype(jnp.float32),
        lax.psum(owned[7].astype(jnp.bfloat16), "ctx").astype(jnp.float32),
    )
    return (
        result.reshape(batch, frames, width),
        input_grad.reshape(batch, frames, width),
        gain_total,
        owned[0],
        owned[1],
        owned[2],
        owned[3],
        owned[4],
        owned[5],
        kernel_total,
        jnp.stack([scale_sum, bias_sum]),
        owned[6],
        owned[7],
    )


def solution(mesh):
    placed = (
        P("fsdp", "ctx", None),
        P("fsdp", "ctx", None),
        P("fsdp"),
        P(),
        P("fsdp", "tp"),
        P("fsdp", "tp"),
        P("fsdp", None, "tp"),
        P("fsdp", "tp"),
        P("fsdp", None, "tp"),
        P("fsdp", "tp"),
        P(None, "tp"),
        P(None, "tp"),
        P("fsdp", "tp"),
        P("fsdp", "tp"),
    )
    return jax.shard_map(
        per_device,
        mesh=mesh,
        in_specs=placed,
        out_specs=(
            P("fsdp", "ctx", None),
            P("fsdp", "ctx", None),
            P(),
            P("fsdp", "tp"),
            P("fsdp", "tp"),
            P("fsdp", None, "tp"),
            P("fsdp", "tp"),
            P("fsdp", None, "tp"),
            P("fsdp", "tp"),
            P(None, "tp"),
            P(None, "tp"),
            P("fsdp", "tp"),
            P("fsdp", "tp"),
        ),
        check_vma=False,
    )
```

profile of v0, /device:TPU:0, one launch (start us, length us, event | category | flops | bytes accessed | tf_op | source)
XLA Modules:
  0.0 1221.6 jit_solution(15383758015206890385)
XLA Ops:
  11.6 28.7 %all-gather.6.cloned.1.call-done = bf16[512,1024]{1,0:T(8,128)(2,1)} async-done(((bf16[128,1024]{1,0:T(8,128)(2,1)}), bf16[512,1024]{1,0:T(8,128)(2,1)}) %all-gather.6.cloned.1.call-update) | async-done | bytes 1048592 | tf_op jit(solution)/shard_map/all_gather | solution.py:157
  40.3 5.1 multiply_convert_fusion.2
  45.4 23.9 %all-gather.8.cloned.1.call-done = bf16[512,1024]{1,0:T(8,128)(2,1)} async-done(((bf16[128,1024]{1,0:T(8,128)(2,1)}), bf16[512,1024]{1,0:T(8,128)(2,1)}) %all-gather.8.cloned.1.call-update) | async-done | bytes 1048592 | tf_op jit(solution)/shard_map/all_gather | solution.py:158
  69.3 4.1 convolution_convert_fusion.10
  74.3 17.5 %all_gather.29 = bf16[512,3,256]{0,2,1:T(8,128)(2,1)S(1)} all-gather(bf16[128,3,256]{0,2,1:T(8,128)(2,1)S(1)} %copy.27), channel_id=1, replica_groups=mesh['fsdp'=4,'ctx'=4,'tp'=2] {'fsdp'}, dimensions={0}, use_global_device_ids=true | all-gather | bytes 983040 | tf_op jit(solution)/shard_map/all_gather | solution.py:159
  91.8 21.4 %all-reduce.20.cloned.1.call-done = bf16[1024,512]{1,0:T(8,128)(2,1)} async-done(((bf16[1024,512]{1,0:T(8,128)(2,1)}), bf16[1024,512]{1,0:T(8,128)(2,1)}) %all-reduce.20.cloned.1.call-update) | async-done | bytes 1048592 | tf_op jit(solution)/shard_map/psum | solution.py:51
  119.6 14.3 %all_gather.31 = bf16[512,256]{1,0:T(8,128)(2,1)S(1)} all-gather(bf16[128,256]{1,0:T(8,128)(2,1)S(1)} %copy-done.69), channel_id=1, replica_groups=mesh['fsdp'=4,'ctx'=4,'tp'=2] {'fsdp'}, dimensions={0}, use_global_device_ids=true | all-gather | bytes 327680 | tf_op jit(solution)/shard_map/all_gather | solution.py:160
  134.0 19.6 %all-gather.10.cloned.1.call-done = bf16[1,4096,512]{1,2,0:T(8,128)(2,1)} async-done(((bf16[1,1024,512]{1,2,0:T(8,128)(2,1)}), bf16[1,4096,512]{1,2,0:T(8,128)(2,1)}) %all-gather.10.cloned.1.call-update) | async-done | bytes 4194320 | tf_op jit(solution)/shard_map/all_gather | solution.py:190
  153.5 4.1 fusion.240
  157.6 23.1 %select_reduce_fusion = (f32[4,1024]{1,0:T(4,128)S(1)}, f32[4,1024,4096]{2,1,0:T(8,128)}) fusion(pred[4096]{0:T(1024)(128)(4,1)S(1)} %iota_compare_fusion, bf16[4096,4,64]{0,2,1:T(8,128)(2,1)S(1)} %bitcast.233, f32[1024,4,32]{0,2,1:T(8,128)S(1)} %get-tuple-element.156, f32[1024,4,32]{0,2,1:T(8,128)S(1)} %get-tuple-element.155), kind=kOutput, calls=%fused_computation.6 | convolution fusion | flops 2181820416 | bytes 70275072 | tf_op jit(solution)/shard_map/while/body/eval_jaxpr/fhe,lhe->hfl/dot_general | solution.py:97
  180.8 21.4 %fusion = f32[4,1024]{1,0:T(4,128)S(1)} fusion(f32[4,1024,4096]{2,1,0:T(8,128)} %get-tuple-element.214, f32[4,1024]{1,0:T(4,128)S(1)} %get-tuple-element.213, pred[4096]{0:T(1024)(128)(4,1)S(1)} %iota_compare_fusion), kind=kLoop, calls=%fused_computation.5 | loop fusion | flops 50327552 | bytes 67145728 | tf_op jit(solution)/shard_map/while/body/eval_jaxpr/reduce_sum | solution.py:108
  202.2 24.0 %fusion.33 = bf16[4,64,1024]{2,1,0:T(8,128)(2,1)S(1)} fusion(bf16[4096,4,64]{0,2,1:T(8,128)(2,1)S(1)} %bitcast.241, f32[4,1024,4096]{2,1,0:T(8,128)} %get-tuple-element.214, f32[4,1024]{1,0:T(4,128)S(1)} %fusion, f32[4,1024]{1,0:T(4,128)S(1)} %get-tuple-element.213, pred[4096]{0:T(1024)(128)(4,1)S(1)} %iota_compare_fusion), kind=kOutput, calls=%fused_computation.222 | convolution fusion | flops 2214854656 | bytes 69767168 | tf_op jit(solution)/shard_map/while/body/eval_jaxpr/hfl,lhe->fhe/dot_general | solution.py:110
  227.8 16.0 %all_gather.32 = bf16[512,2,256]{2,0,1:T(8,128)(2,1)S(1)} all-gather(bf16[128,2,256]{2,0,1:T(8,128)(2,1)S(1)} %copy.28), channel_id=1, replica_groups=mesh['fsdp'=4,'ctx'=4,'tp'=2] {'fsdp'}, dimensions={0}, use_global_device_ids=true | all-gather | bytes 655360 | tf_op jit(solution)/shard_map/all_gather | solution.py:161
  245.1 22.8 %all-reduce.22.cloned.1.call-done = bf16[1024,512]{1,0:T(8,128)(2,1)} async-done(((bf16[1024,512]{1,0:T(8,128)(2,1)}), bf16[1024,512]{1,0:T(8,128)(2,1)}) %all-reduce.22.cloned.1.call-update) | async-done | bytes 1048592 | tf_op jit(solution)/shard_map/psum | solution.py:51
  276.0 15.4 %all_gather.33 = bf16[512,256]{1,0:T(8,128)(2,1)} all-gather(bf16[128,256]{1,0:T(8,128)(2,1)S(1)} %copy-done.70), channel_id=1, replica_groups=mesh['fsdp'=4,'ctx'=4,'tp'=2] {'fsdp'}, dimensions={0}, use_global_device_ids=true | all-gather | bytes 327680 | tf_op jit(solution)/shard_map/all_gather | solution.py:162
  292.3 9.3 fusion.64
  301.6 32.1 %all-reduce.8 = (f32[256]{0:T(256)S(1)}, f32[]{:T(128)}, f32[256]{0:T(256)S(1)}) all-reduce(f32[256]{0:T(256)} %get-tuple-element.109, f32[]{:T(128)} %fusion.202, f32[256]{0:T(256)} %get-tuple-element.108), channel_id=1, replica_groups=mesh['fsdp'=4,'ctx'=4,'tp'=2] {'fsdp','ctx'}, use_global_device_ids=true, to_apply=%region_11.12 | all-reduce | flops 513 | bytes 4104 | tf_op jit(solution)/shard_map/psum | solution.py:211
  334.9 2.8 convolution_convert_fusion.8
  339.3 35.0 %all-reduce.24.cloned.1.call-done = bf16[1024,512]{1,0:T(8,128)(2,1)} async-done(((bf16[1024,512]{1,0:T(8,128)(2,1)}), bf16[1024,512]{1,0:T(8,128)(2,1)}) %all-reduce.24.cloned.1.call-update) | async-done | bytes 1048592 | tf_op jit(solution)/shard_map/psum | solution.py:51
  377.6 26.3 %all-gather.12.cloned.1.call-done = bf16[512,1024]{1,0:T(8,128)(2,1)} async-done(((bf16[128,1024]{1,0:T(8,128)(2,1)}), bf16[512,1024]{1,0:T(8,128)(2,1)}) %all-gather.12.cloned.1.call-update) | async-done | bytes 1048592 | tf_op jit(solution)/shard_map/all_gather | solution.py:163
  403.9 6.1 multiply_convert_fusion.1
  410.0 22.9 %all-gather.14.cloned.1.call-done = bf16[512,1024]{1,0:T(8,128)(2,1)} async-done(((bf16[128,1024]{1,0:T(8,128)(2,1)}), bf16[512,1024]{1,0:T(8,128)(2,1)}) %all-gather.14.cloned.1.call-update) | async-done | bytes 1048592 | tf_op jit(solution)/shard_map/all_gather | solution.py:164
  432.9 4.1 convolution_convert_fusion.7
  437.0 39.6 %all-reduce.26.cloned.1.call-done = bf16[1024,512]{1,0:T(8,128)(2,1)} async-done(((bf16[1024,512]{1,0:T(8,128)(2,1)}), bf16[1024,512]{1,0:T(8,128)(2,1)}) %all-reduce.26.cloned.1.call-update) | async-done | bytes 1048592 | tf_op jit(solution)/shard_map/psum | solution.py:51
  485.5 2.5 fusion.11
  492.0 40.0 %all-reduce.28.cloned.1.call-done = bf16[1024,512]{1,0:T(8,128)(2,1)} async-done(((bf16[1024,512]{1,0:T(8,128)(2,1)}), bf16[1024,512]{1,0:T(8,128)(2,1)}) %all-reduce.28.cloned.1.call-update) | async-done | bytes 1048592 | tf_op jit(solution)/shard_map/psum | solution.py:51
  532.0 2.6 fusion.26
  542.2 33.7 %all-reduce.7 = (f32[256]{0:T(256)}, f32[256]{0:T(256)}) all-reduce(f32[256]{0:T(256)} %get-tuple-element.217, f32[256]{0:T(256)} %reduce_sum.647), channel_id=1, replica_groups=mesh['fsdp'=4,'ctx'=4,'tp'=2] {'fsdp','ctx'}, use_global_device_ids=true, to_apply=%region_30.31 | all-reduce | flops 512 | bytes 4096 | tf_op jit(solution)/shard_map/psum | solution.py:241
  577.5 5.4 fusion.115
  584.2 3.0 collective-permute-start.3
  588.1 9.3 fusion.67
  600.7 38.1 %all-reduce.30.cloned.1.call-done = bf16[1024,512]{1,0:T(8,128)(2,1)} async-done(((bf16[1024,512]{1,0:T(8,128)(2,1)}), bf16[1024,512]{1,0:T(8,128)(2,1)}) %all-reduce.30.cloned.1.call-update) | async-done | bytes 1048592 | tf_op jit(solution)/shard_map/psum | solution.py:51
  640.7 2.3 fusion.28
  645.5 23.9 %fusion.6 = bf16[4,64,4096]{2,1,0:T(8,128)(2,1)S(1)} fusion(bf16[1024,4,64]{0,2,1:T(8,128)(2,1)S(1)} %bitcast.237, f32[4,1024,4096]{2,1,0:T(8,128)} %get-tuple-element.214, f32[4,1024]{1,0:T(4,128)S(1)} %log_add_fusion, pred[4096]{0:T(1024)(128)(4,1)S(1)} %iota_compare_fusion), kind=kOutput, calls=%fused_computation.45 | convolution fusion | flops 2198863872 | bytes 69750784 | tf_op jit(solution)/shard_map/while/body/eval_jaxpr/hfl,fhe->lhe/dot_general | solution.py:124
  669.4 45.1 %multiply_reduce_fusion = (f32[4,1024]{1,0:T(4,128)S(1)}, f32[4,1024,4096]{2,1,0:T(8,128)}) fusion(f32[4,1024,4096]{2,1,0:T(8,128)} %get-tuple-element.214, f32[4,1024]{1,0:T(4,128)S(1)} %log_add_fusion, pred[4096]{0:T(1024)(128)(4,1)S(1)} %iota_compare_fusion, bf16[1024,4,64]{0,2,1:T(8,128)(2,1)S(1)} %bitcast.238, bf16[4096,4,64]{0,2,1:T(8,128)(2,1)S(1)} %bitcast.242), kind=kOutput, calls=%fused_computation.1 | convolution fusion | flops 2214588416 | bytes 136876032 | tf_op jit(solution)/shard_map/while/body/eval_jaxpr/fhe,lhe->hfl/dot_general | solution.py:119
  714.5 2.5 copy.30
  717.0 52.7 %multiply_convert_fusion = bf16[4,1024,4096]{2,1,0:T(8,128)(2,1)} fusion(f32[4,1024,4096]{2,1,0:T(8,128)} %get-tuple-element.220, f32[4,1024,4096]{2,1,0:T(8,128)} %get-tuple-element.214, f32[4,1024]{1,0:T(4,128)S(1)} %get-tuple-element.219, f32[4,1024]{1,0:T(4,128)S(1)} %log_add_fusion, pred[4096]{0:T(1024)(128)(4,1)S(1)} %iota_compare_fusion), kind=kLoop, calls=%fused_computation | loop fusion | flops 83886080 | bytes 167809024 | tf_op jit(solution)/shard_map/while/body/eval_jaxpr/convert_element_type | solution.py:121
  769.7 13.8 %convolution_convert_fusion = bf16[4,64,4096]{2,1,0:T(8,128)(2,1)S(1)} fusion(bf16[4,1024,4096]{2,1,0:T(8,128)(2,1)} %multiply_convert_fusion, f32[1024,4,32]{0,2,1:T(8,128)S(1)} %copy-done.36, f32[1024,4,32]{0,2,1:T(8,128)S(1)} %copy-done.34), kind=kOutput, calls=%fused_computation.46 | convolution fusion | flops 2149318656 | bytes 36700160 | tf_op jit(solution)/shard_map/while/body/eval_jaxpr/hfl,fhe->lhe/dot_general | solution.py:123
  783.5 2.5 copy.29
  786.0 4.5 pad_maximum_fusion
  792.1 17.0 %fusion.32 = f32[1,1024,4,64]{1,3,2,0:T(8,128)S(1)} fusion(bf16[4096,4,64]{0,2,1:T(8,128)(2,1)S(1)} %bitcast.234, bf16[4,1024,4096]{2,1,0:T(8,128)(2,1)} %multiply_convert_fusion), kind=kOutput, calls=%fused_computation.188 | convolution fusion | flops 2147745792 | bytes 36700160 | tf_op jit(solution)/shard_map/while/body/eval_jaxpr/hfl,lhe->fhe/dot_general | solution.py:122
  809.1 26.2 %reduce-scatter.10.cloned.1.call-done = bf16[1,1024,512]{2,1,0:T(8,128)(2,1)} async-done(((bf16[1,4096,512]{2,1,0:T(8,128)(2,1)}), bf16[1,1024,512]{2,1,0:T(8,128)(2,1)}) %reduce-scatter.10.cloned.1.call-update) | async-done | bytes 1048592 | tf_op jit(solution)/shard_map/reduce_scatter | solution.py:283
  840.2 3.4 bitcast_convert_fusion
  843.6 40.2 %all-reduce.32.cloned.1.call-done = bf16[1024,512]{1,0:T(8,128)(2,1)} async-done(((bf16[1024,512]{1,0:T(8,128)(2,1)}), bf16[1024,512]{1,0:T(8,128)(2,1)}) %all-reduce.32.cloned.1.call-update) | async-done | bytes 1048592 | tf_op jit(solution)/shard_map/psum | solution.py:51
  894.3 2.3 convolution_convert_fusion.5
  896.7 3.1 convolution_convert_fusion.14
  900.0 4.0 convolution_convert_fusion.2
  904.1 4.7 convolution_convert_fusion.1
  909.1 3.4 convolution_convert_fusion.13
  912.6 2.9 convolution_convert_fusion.15
  915.7 3.3 convolution_convert_fusion.11
  919.2 4.7 convolution_convert_fusion.4
  924.0 4.0 convolution_convert_fusion.3
  933.3 3.6 all-reduce.34.cloned.1.call-done
  938.8 20.8 %reduce-scatter.22.cloned.1.call-done = bf16[128,256]{1,0:T(8,128)(2,1)} async-done(((bf16[512,256]{1,0:T(8,128)(2,1)}), bf16[128,256]{1,0:T(8,128)(2,1)}) %reduce-scatter.22.cloned.1.call-update) | async-done | bytes 65552 | tf_op jit(solution)/shard_map/reduce_scatter | solution.py:334
  959.5 27.7 %reduce-scatter.24.cloned.1.call-done = bf16[128,1024]{1,0:T(8,128)(2,1)} async-done(((bf16[512,1024]{1,0:T(8,128)(2,1)}), bf16[128,1024]{1,0:T(8,128)(2,1)}) %reduce-scatter.24.cloned.1.call-update) | async-done | bytes 262160 | tf_op jit(solution)/shard_map/reduce_scatter | solution.py:337
  987.2 27.9 %reduce-scatter.26.cloned.1.call-done = bf16[128,1024]{1,0:T(8,128)(2,1)} async-done(((bf16[512,1024]{1,0:T(8,128)(2,1)}), bf16[128,1024]{1,0:T(8,128)(2,1)}) %reduce-scatter.26.cloned.1.call-update) | async-done | bytes 262160 | tf_op jit(solution)/shard_map/reduce_scatter | solution.py:340
  1015.2 22.5 %reduce-scatter.20.cloned.1.call-done = bf16[128,2,256]{2,0,1:T(8,128)(2,1)} async-done(((bf16[512,2,256]{2,0,1:T(8,128)(2,1)}), bf16[128,2,256]{2,0,1:T(8,128)(2,1)}) %reduce-scatter.20.cloned.1.call-update) | async-done | bytes 131088 | tf_op jit(solution)/shard_map/reduce_scatter | solution.py:331
  1037.7 21.1 %reduce-scatter.18.cloned.1.call-done = bf16[128,256]{1,0:T(8,128)(2,1)} async-done(((bf16[512,256]{1,0:T(8,128)(2,1)}), bf16[128,256]{1,0:T(8,128)(2,1)}) %reduce-scatter.18.cloned.1.call-update) | async-done | bytes 65552 | tf_op jit(solution)/shard_map/reduce_scatter | solution.py:328
  1058.8 23.5 %reduce-scatter.16.cloned.1.call-done = bf16[128,3,256]{2,0,1:T(8,128)(2,1)} async-done(((bf16[512,3,256]{2,0,1:T(8,128)(2,1)}), bf16[128,3,256]{2,0,1:T(8,128)(2,1)}) %reduce-scatter.16.cloned.1.call-update) | async-done | bytes 196624 | tf_op jit(solution)/shard_map/reduce_scatter | solution.py:325
  1082.3 29.1 %reduce-scatter.12.cloned.1.call-done = bf16[128,1024]{1,0:T(8,128)(2,1)} async-done(((bf16[512,1024]{1,0:T(8,128)(2,1)}), bf16[128,1024]{1,0:T(8,128)(2,1)}) %reduce-scatter.12.cloned.1.call-update) | async-done | bytes 262160 | tf_op jit(solution)/shard_map/reduce_scatter | solution.py:319
  1111.5 28.1 %reduce-scatter.14.cloned.1.call-done = bf16[128,1024]{1,0:T(8,128)(2,1)} async-done(((bf16[512,1024]{1,0:T(8,128)(2,1)}), bf16[128,1024]{1,0:T(8,128)(2,1)}) %reduce-scatter.14.cloned.1.call-update) | async-done | bytes 262160 | tf_op jit(solution)/shard_map/reduce_scatter | solution.py:322
  1141.0 59.7 %all-reduce.6 = (f32[5,512]{1,0:T(8,128)}, f32[31,256]{1,0:T(8,128)}) all-reduce(f32[5,512]{1,0:T(8,128)S(1)} %stack.128, f32[31,256]{1,0:T(8,128)S(1)} %stack.160), channel_id=1, replica_groups=mesh['fsdp'=4,'ctx'=4,'tp'=2] {'fsdp','ctx'}, use_global_device_ids=true, to_apply=%region_47.48 | all-reduce | flops 10496 | bytes 83968 | tf_op jit(solution)/shard_map/psum | solution.py:307
  1200.7 3.3 add_bitcast_fusion
  (449 shorter events, 96.4 us)
Async XLA Ops:
  7.2 33.1 %all-gather.6.cloned.1.call-start = ((), (), s32[]{:S(2)}) async-start(), calls=%async_computation.9 | async-start | bytes 1310720 | tf_op jit(solution)/shard_map/all_gather | solution.py:157
  7.9 61.3 %all-gather.8.cloned.1.call-start = ((), (), s32[]{:S(2)}) async-start(), calls=%async_computation.10 | async-start | bytes 1310720 | tf_op jit(solution)/shard_map/all_gather | solution.py:158
  8.7 104.4 %all-reduce.20.cloned.1.call-start = ((), (), s32[]{:S(2)}) async-start(), calls=%async_computation.11 | async-start | bytes 2097152 | tf_op jit(solution)/shard_map/psum | solution.py:51
  10.6 34.8 %copy-start.65 = (f32[1024]{0:T(1024)}, f32[1024]{0:T(1024)S(1)}, u32[]{:S(2)}) copy-start(f32[1024]{0:T(1024)S(1)} %broadcast_multiply_fusion.4) | copy-start | bytes 12292
  11.0 34.4 %copy-start.83 = (f32[1024]{0:T(1024)}, f32[1024]{0:T(1024)S(1)}, u32[]{:S(2)}) copy-start(f32[1024]{0:T(1024)S(1)} %multiply_reduce_fusion.6) | copy-start | bytes 12292
  11.6 104.2 %copy-start.75 = (f32[1,512]{1,0:T(1,128)}, f32[1,512]{1,0:T(1,128)S(1)}, u32[]{:S(2)}) copy-start(f32[1,512]{1,0:T(1,128)S(1)} %get-tuple-element.202) | copy-start | bytes 6148
  11.6 631.4 %copy-start.77 = (f32[1,512]{1,0:T(1,128)}, f32[1,512]{1,0:T(1,128)S(1)}, u32[]{:S(2)}) copy-start(f32[1,512]{1,0:T(1,128)S(1)} %get-tuple-element.201) | copy-start | bytes 6148
  73.4 80.1 %all-gather.10.cloned.1.call-start = ((), (), s32[]{:S(2)}) async-start(), calls=%async_computation.12 | async-start | bytes 5242880 | tf_op jit(solution)/shard_map/all_gather | solution.py:190
  74.2 43.1 %copy-start.43 = (f32[1024,32]{0,1:T(8,128)}, f32[1024,32]{0,1:T(8,128)S(1)}, u32[]{:S(2)}) copy-start(f32[1024,32]{0,1:T(8,128)S(1)} %get-tuple-element.205) | copy-start | bytes 393220
  74.2 43.1 %copy-start.45 = (f32[1024,32]{0,1:T(8,128)}, f32[1024,32]{0,1:T(8,128)S(1)}, u32[]{:S(2)}) copy-start(f32[1024,32]{0,1:T(8,128)S(1)} %get-tuple-element.206) | copy-start | bytes 393220
  117.6 40.0 %copy-start.33 = (f32[1024,4,32]{0,2,1:T(8,128)}, f32[1024,4,32]{0,2,1:T(8,128)S(1)}, u32[]{:S(2)}) copy-start(f32[1024,4,32]{0,2,1:T(8,128)S(1)} %get-tuple-element.155) | copy-start | bytes 1572868
  117.6 40.0 %copy-start.35 = (f32[1024,4,32]{0,2,1:T(8,128)}, f32[1024,4,32]{0,2,1:T(8,128)S(1)}, u32[]{:S(2)}) copy-start(f32[1024,4,32]{0,2,1:T(8,128)S(1)} %get-tuple-element.156) | copy-start | bytes 1572868
  118.9 149.0 %all-reduce.22.cloned.1.call-start = ((), (), s32[]{:S(2)}) async-start(), calls=%async_computation.13 | async-start | bytes 2097152 | tf_op jit(solution)/shard_map/psum | solution.py:51
  226.2 43.9 %copy-start.41 = (bf16[4,64,1024]{2,1,0:T(8,128)(2,1)}, bf16[4,64,1024]{2,1,0:T(8,128)(2,1)S(1)}, u32[]{:S(2)}) copy-start(bf16[4,64,1024]{2,1,0:T(8,128)(2,1)S(1)} %fusion.33) | copy-start | bytes 1572868
  227.7 146.6 %all-reduce.24.cloned.1.call-start = ((), (), s32[]{:S(2)}) async-start(), calls=%async_computation.14 | async-start | bytes 2097152 | tf_op jit(solution)/shard_map/psum | solution.py:51
  244.4 331.5 %copy-start.95 = (f32[1,256]{1,0:T(1,128)}, f32[1,256]{1,0:T(1,128)S(1)}, u32[]{:S(2)}) copy-start(f32[1,256]{1,0:T(1,128)S(1)} %get-tuple-element.209) | copy-start | bytes 3076
  245.1 47.0 %copy-start.97 = (f32[1,256]{1,0:T(1,128)}, f32[1,256]{1,0:T(1,128)S(1)}, u32[]{:S(2)}) copy-start(f32[1,256]{1,0:T(1,128)S(1)} %get-tuple-element.170) | copy-start | bytes 3076
  245.1 47.0 %copy-start.99 = (f32[1,256]{1,0:T(1,128)}, f32[1,256]{1,0:T(1,128)S(1)}, u32[]{:S(2)}) copy-start(f32[1,256]{1,0:T(1,128)S(1)} %get-tuple-element.171) | copy-start | bytes 3076
  245.1 47.0 %copy-start.101 = (f32[1,256]{1,0:T(1,128)}, f32[1,256]{1,0:T(1,128)S(1)}, u32[]{:S(2)}) copy-start(f32[1,256]{1,0:T(1,128)S(1)} %get-tuple-element.172) | copy-start | bytes 3076
  245.1 47.0 %copy-start.103 = (f32[1,256]{1,0:T(1,128)}, f32[1,256]{1,0:T(1,128)S(1)}, u32[]{:S(2)}) copy-start(f32[1,256]{1,0:T(1,128)S(1)} %get-tuple-element.173) | copy-start | bytes 3076
  270.1 372.9 %copy-start = (f32[1024,512]{1,0:T(8,128)}, f32[1024,512]{1,0:T(8,128)S(1)}, u32[]{:S(2)}) copy-start(f32[1024,512]{1,0:T(8,128)S(1)} %get-tuple-element.143) | copy-start | bytes 6291460
  270.1 372.9 %copy-start.58 = (f32[1024]{0:T(1024)}, f32[1024]{0:T(1024)S(1)}, u32[]{:S(2)}) copy-start(f32[1024]{0:T(1024)S(1)} %broadcast_multiply_fusion.2) | copy-start | bytes 12292
  270.6 372.4 %copy-start.73 = (f32[1024]{0:T(1024)}, f32[1024]{0:T(1024)S(1)}, u32[]{:S(2)}) copy-start(f32[1024]{0:T(1024)S(1)} %fusion.199) | copy-start | bytes 12292
  273.1 304.3 %copy-start.14 = (bf16[1,1024,256]{2,1,0:T(8,128)(2,1)}, bf16[1,1024,256]{2,1,0:T(8,128)(2,1)S(1)}, u32[]{:S(2)}) copy-start(bf16[1,1024,256]{2,1,0:T(8,128)(2,1)S(1)} %fusion.127) | copy-start | bytes 1572868
  273.2 18.9 %collective-permute-start = (bf16[1,15,256]{2,1,0:T(8,128)(2,1)S(1)}, bf16[1,15,256]{2,1,0:T(8,128)(2,1)S(1)}, u32[]{:S(2)}, u32[]{:S(2)}) collective-permute-start(bf16[1,15,256]{2,1,0:T(8,128)(2,1)S(1)} %get-tuple-element.163), channel_id=1, source_target_pairs={{0,2},{2,4},{4,6},{1,3},{3,5},{5,7},{8,10},{10,12},{12,14},{9,11},... | collective-permute-start | bytes 23048 | tf_op jit(solution)/shard_map/ppermute | solution.py:20
  274.7 17.4 %collective-permute-start.1 = (bf16[1,15,256]{2,1,0:T(8,128)(2,1)S(1)}, bf16[1,15,256]{2,1,0:T(8,128)(2,1)S(1)}, u32[]{:S(2)}, u32[]{:S(2)}) collective-permute-start(bf16[1,15,256]{2,1,0:T(8,128)(2,1)S(1)} %get-tuple-element.164), channel_id=1, source_target_pairs={{2,0},{4,2},{6,4},{3,1},{5,3},{7,5},{10,8},{12,10},{14,12},{11,9},... | collective-permute-start | bytes 23048 | tf_op jit(solution)/shard_map/ppermute | solution.py:22
  292.1 45.6 %copy-start.62 = (bf16[1,15,256]{2,1,0:T(8,128)(2,1)}, bf16[1,15,256]{2,1,0:T(8,128)(2,1)S(1)}, u32[]{:S(2)}) copy-start(bf16[1,15,256]{2,1,0:T(8,128)(2,1)S(1)} %collective-permute-done) | copy-start | bytes 23044
  292.1 285.4 %copy-start.60 = (bf16[1,15,256]{2,1,0:T(8,128)(2,1)}, bf16[1,15,256]{2,1,0:T(8,128)(2,1)S(1)}, u32[]{:S(2)}) copy-start(bf16[1,15,256]{2,1,0:T(8,128)(2,1)S(1)} %collective-permute-done.1) | copy-start | bytes 23044
  337.7 66.2 %all-gather.12.cloned.1.call-start = ((), (), s32[]{:S(2)}) async-start(), calls=%async_computation.15 | async-start | bytes 1310720 | tf_op jit(solution)/shard_map/all_gather | solution.py:163
  338.5 94.4 %all-gather.14.cloned.1.call-start = ((), (), s32[]{:S(2)}) async-start(), calls=%async_computation.16 | async-start | bytes 1310720 | tf_op jit(solution)/shard_map/all_gather | solution.py:164
  339.2 137.4 %all-reduce.26.cloned.1.call-start = ((), (), s32[]{:S(2)}) async-start(), calls=%async_computation.17 | async-start | bytes 2097152 | tf_op jit(solution)/shard_map/psum | solution.py:51
  375.8 160.8 %copy-start.67 = (f32[1024]{0:T(1024)}, f32[1024]{0:T(1024)S(1)}, u32[]{:S(2)}) copy-start(f32[1024]{0:T(1024)S(1)} %broadcast_multiply_fusion.1) | copy-start | bytes 12292
  377.6 159.1 %copy-start.81 = (f32[1024]{0:T(1024)}, f32[1024]{0:T(1024)S(1)}, u32[]{:S(2)}) copy-start(f32[1024]{0:T(1024)S(1)} %fusion.200) | copy-start | bytes 12292
  437.0 95.0 %all-reduce.28.cloned.1.call-start = ((), (), s32[]{:S(2)}) async-start(), calls=%async_computation.18 | async-start | bytes 2097152 | tf_op jit(solution)/shard_map/psum | solution.py:51
  483.8 52.9 %copy-start.93 = (f32[1024]{0:T(1024)}, f32[1024]{0:T(1024)S(1)}, u32[]{:S(2)}) copy-start(f32[1024]{0:T(1024)S(1)} %negate_multiply_fusion.4) | copy-start | bytes 12292
  491.7 147.0 %all-reduce.30.cloned.1.call-start = ((), (), s32[]{:S(2)}) async-start(), calls=%async_computation.19 | async-start | bytes 2097152 | tf_op jit(solution)/shard_map/psum | solution.py:51
  540.2 47.8 %copy-start.98 = (f32[1,256]{1,0:T(1,128)S(1)}, f32[1,256]{1,0:T(1,128)}, u32[]{:S(2)}) copy-start(f32[1,256]{1,0:T(1,128)} %copy-done.97) | copy-start | bytes 3076
  540.2 47.8 %copy-start.100 = (f32[1,256]{1,0:T(1,128)S(1)}, f32[1,256]{1,0:T(1,128)}, u32[]{:S(2)}) copy-start(f32[1,256]{1,0:T(1,128)} %copy-done.99) | copy-start | bytes 3076
  540.2 47.8 %copy-start.102 = (f32[1,256]{1,0:T(1,128)S(1)}, f32[1,256]{1,0:T(1,128)}, u32[]{:S(2)}) copy-start(f32[1,256]{1,0:T(1,128)} %copy-done.101) | copy-start | bytes 3076
  540.2 47.8 %copy-start.104 = (f32[1,256]{1,0:T(1,128)S(1)}, f32[1,256]{1,0:T(1,128)}, u32[]{:S(2)}) copy-start(f32[1,256]{1,0:T(1,128)} %copy-done.103) | copy-start | bytes 3076
  540.2 47.8 %copy-start.106 = (f32[1,256]{1,0:T(1,128)S(1)}, f32[1,256]{1,0:T(1,128)}, u32[]{:S(2)}) copy-start(f32[1,256]{1,0:T(1,128)} %get-tuple-element.174) | copy-start | bytes 3076
  540.3 47.8 %copy-start.108 = (f32[1,256]{1,0:T(1,128)S(1)}, f32[1,256]{1,0:T(1,128)}, u32[]{:S(2)}) copy-start(f32[1,256]{1,0:T(1,128)} %get-tuple-element.175) | copy-start | bytes 3076
  582.9 4.3 collective-permute-start.2
  584.2 3.8 collective-permute-start.3
  600.6 234.7 %reduce-scatter.10.cloned.1.call-start = ((), (), s32[]{:S(2)}) async-start(), calls=%async_computation.20 | async-start | bytes 5242880 | tf_op jit(solution)/shard_map/reduce_scatter | solution.py:283
  717.0 52.7 %copy-start.34 = (f32[1024,4,32]{0,2,1:T(8,128)S(1)}, f32[1024,4,32]{0,2,1:T(8,128)}, u32[]{:S(2)}) copy-start(f32[1024,4,32]{0,2,1:T(8,128)} %copy-done.33) | copy-start | bytes 1572868
  717.0 52.7 %copy-start.36 = (f32[1024,4,32]{0,2,1:T(8,128)S(1)}, f32[1024,4,32]{0,2,1:T(8,128)}, u32[]{:S(2)}) copy-start(f32[1024,4,32]{0,2,1:T(8,128)} %copy-done.35) | copy-start | bytes 1572868
  790.5 93.3 %all-reduce.32.cloned.1.call-start = ((), (), s32[]{:S(2)}) async-start(), calls=%async_computation.21 | async-start | bytes 2097152 | tf_op jit(solution)/shard_map/psum | solution.py:51
  840.2 43.7 %copy-start.3 = (f32[1024,512]{1,0:T(8,128)S(1)}, f32[1024,512]{1,0:T(8,128)}, u32[]{:S(2)}) copy-start(f32[1024,512]{1,0:T(8,128)} %copy-done.2) | copy-start | bytes 6291460
  840.2 43.7 %copy-start.57 = (f32[1024]{0:T(1024)S(1)}, f32[1024]{0:T(1024)}, u32[]{:S(2)}) copy-start(f32[1024]{0:T(1024)} %copy-done.56) | copy-start | bytes 12292
  840.2 43.7 %copy-start.76 = (f32[1,512]{1,0:T(1,128)S(1)}, f32[1,512]{1,0:T(1,128)}, u32[]{:S(2)}) copy-start(f32[1,512]{1,0:T(1,128)} %copy-done.75) | copy-start | bytes 6148
  843.6 42.2 %copy-start.86 = (f32[1024]{0:T(1024)S(1)}, f32[1024]{0:T(1024)}, u32[]{:S(2)}) copy-start(f32[1024]{0:T(1024)} %copy-done.85) | copy-start | bytes 12292
  843.6 42.3 %copy-start.72 = (f32[1024]{0:T(1024)S(1)}, f32[1024]{0:T(1024)}, u32[]{:S(2)}) copy-start(f32[1024]{0:T(1024)} %copy-done.71) | copy-start | bytes 12292
  843.6 93.3 %all-reduce.34.cloned.1.call-start = ((), (), s32[]{:S(2)}) async-start(), calls=%async_computation.22 | async-start | bytes 2097152 | tf_op jit(solution)/shard_map/psum | solution.py:51
  896.6 62.9 %reduce-scatter.22.cloned.1.call-start = ((), (), s32[]{:S(2)}) async-start(), calls=%async_computation.28 | async-start | bytes 327680 | tf_op jit(solution)/shard_map/reduce_scatter | solution.py:334
  899.9 87.4 %reduce-scatter.24.cloned.1.call-start = ((), (), s32[]{:S(2)}) async-start(), calls=%async_computation.29 | async-start | bytes 1310720 | tf_op jit(solution)/shard_map/reduce_scatter | solution.py:337
  904.0 111.2 %reduce-scatter.26.cloned.1.call-start = ((), (), s32[]{:S(2)}) async-start(), calls=%async_computation.30 | async-start | bytes 1310720 | tf_op jit(solution)/shard_map/reduce_scatter | solution.py:340
  908.8 128.9 %reduce-scatter.20.cloned.1.call-start = ((), (), s32[]{:S(2)}) async-start(), calls=%async_computation.27 | async-start | bytes 655360 | tf_op jit(solution)/shard_map/reduce_scatter | solution.py:331
  912.6 146.2 %reduce-scatter.18.cloned.1.call-start = ((), (), s32[]{:S(2)}) async-start(), calls=%async_computation.26 | async-start | bytes 327680 | tf_op jit(solution)/shard_map/reduce_scatter | solution.py:328
  915.6 166.7 %reduce-scatter.16.cloned.1.call-start = ((), (), s32[]{:S(2)}) async-start(), calls=%async_computation.25 | async-start | bytes 983040 | tf_op jit(solution)/shard_map/reduce_scatter | solution.py:325
  919.1 192.4 %reduce-scatter.12.cloned.1.call-start = ((), (), s32[]{:S(2)}) async-start(), calls=%async_computation.23 | async-start | bytes 1310720 | tf_op jit(solution)/shard_map/reduce_scatter | solution.py:319
  924.0 215.6 %reduce-scatter.14.cloned.1.call-start = ((), (), s32[]{:S(2)}) async-start(), calls=%async_computation.24 | async-start | bytes 1310720 | tf_op jit(solution)/shard_map/reduce_scatter | solution.py:322
  928.1 275.8 %all-reduce.36.cloned.1.call-start = ((), (), s32[]{:S(2)}) async-start(), calls=%async_computation.31 | async-start | bytes 3014656 | tf_op jit(solution)/shard_map/psum | solution.py:349
  936.8 202.8 %copy-start.20 = (bf16[1024,512]{1,0:T(8,128)(2,1)S(1)}, bf16[1024,512]{1,0:T(8,128)(2,1)}, u32[]{:S(2)}) copy-start(bf16[1024,512]{1,0:T(8,128)(2,1)} %all-reduce.34.cloned.1.call-done) | copy-start | bytes 3145732
  (113 other events, 850.9 us)
Sparse Core Ops, SparseCore 0:
  9.6 30.6 all-gather.5
  41.9 27.3 all-gather.7
  73.6 39.5 all-reduce.19
  119.1 34.4 all-gather.9
  227.8 40.0 all-reduce.21
  337.8 36.4 all-reduce.23
  375.9 27.9 all-gather.11
  405.5 27.3 all-gather.13
  437.1 39.4 all-reduce.25
  491.8 40.0 all-reduce.27
  600.7 38.0 all-reduce.29
  790.6 44.5 reduce-scatter.9
  843.7 40.1 all-reduce.31
  896.7 40.0 all-reduce.33
  939.5 19.9 reduce-scatter.21
  961.7 25.5 reduce-scatter.23
  989.4 25.7 reduce-scatter.25
  1017.3 20.3 reduce-scatter.19
  1040.5 18.2 reduce-scatter.17
  1060.9 21.3 reduce-scatter.15
  1084.6 26.7 reduce-scatter.11
  1113.8 25.7 reduce-scatter.13
  1142.4 41.1 all-reduce.35
where the time goes:
time: 1230 us; the launch traced here: 1220 us
  waiting for transfers between devices  593 us (48%)
  matrix products  220 us (18%)
  blocking collectives  189 us (15%)
  other arithmetic  164 us (13%)
  local copies, waits for them, and re-layouts  30.3 us (2%)
  between operations  17 us (1%)
    psum x8, waiting for transfers between devices, tensor_total(): lax.psum(partial_value.astype(jnp.bfloat16), 'tp').astype(jnp.float32)  241 us
    psum x1, blocking collectives, per_device(): lax.psum((gain_terms, kernel_local), ('fsdp', 'ctx'))  59.7 us
    convert_element_type x1, other arithmetic, attend_back(): score_grad = (probs * (probs_grad - center)).astype(jnp.bfloat16)  52.7 us
    dot_general x1, matrix products, attend_back(): jnp.einsum('fhe,lhe->hfl', mixed_grad, values, preferred_element_type=jnp...  45.1 us
    psum x1, blocking collectives, per_device(): lax.psum((jnp.sum(shifted_grad, (0, 1)), jnp.sum(shifted_grad * unit, (0,...  33.7 us
    psum x1, blocking collectives, per_device(): lax.psum((jnp.sum(live_cube * filtered, (0, 1)), jnp.sum(live_cube * filt...  32.1 us
    reduce_scatter x1, waiting for transfers between devices, per_device(): lax.psum_scatter(weight_grads[0].astype(jnp.bfloat16), 'fsdp', scatter_di...  29.1 us
    all_gather x1, waiting for transfers between devices, per_device(): lax.all_gather(feed_up, 'fsdp', axis=0, tiled=True)  28.7 us
  transfers between devices with their start and end apart: 27, of which 23 were waited for; matrix products, arithmetic and copies ran while one was open for 6% of the time, Pallas kernels for 0%

commit v1 on v0

--- a/solution.py
+++ b/solution.py
@@ -48,7 +48,9 @@
 
 
 def tensor_total(partial_value):
-    return lax.psum(partial_value.astype(jnp.bfloat16), "tp").astype(jnp.float32)
+    return jnp.sum(lax.all_gather(partial_value.astype(jnp.bfloat16), "tp"), axis=0).astype(
+        jnp.float32
+    )
 
 
 def product_rows(left, right):

time: 1230 us -> 1170 us (0.951)
  waiting for transfers between devices: 593 us -> 522 us
  other arithmetic: 164 us -> 180 us
    psum x8 -> x0, waiting for transfers between devices: 241 us -> none  [tensor_total(): lax.psum(partial_value.astype(jnp.bfloat16), 'tp').astype(jnp.float32)]
    all_gather x0 -> x8, waiting for transfers between devices: none -> 194 us  [tensor_total(): lax.all_gather(partial_value.astype(jnp.bfloat16), 'tp')]
    reduce_scatter x1, waiting for transfers between devices: 27.7 us -> 4.11 us  [per_device(): lax.psum_scatter(weight_grads[6].astype(jnp.bfloat16), 'fsdp', scatter_di...]
    reduce_sum x0 -> x8, other arithmetic: none -> 20.9 us  [tensor_total(): jnp.sum(lax.all_gather(partial_value.astype(jnp.bfloat16), 'tp'), axis=0)]
  transfers between devices with their start and end apart: 27 -> 27, of which waited for: 23 -> 23; matrix products, arithmetic and copies ran while one was open for 6% -> 8% of each run, Pallas kernels for 0% -> 0%
where the time goes in v1:
time: 1170 us; the launch traced here: 1160 us
  waiting for transfers between devices  522 us (45%)
  matrix products  213 us (18%)
  blocking collectives  187 us (16%)
  other arithmetic  180 us (15%)
  local copies, waits for them, and re-layouts  32.7 us (3%)
  between operations  17.8 us (2%)
    all_gather x8, waiting for transfers between devices, tensor_total(): lax.all_gather(partial_value.astype(jnp.bfloat16), 'tp')  194 us
    psum x1, blocking collectives, per_device(): lax.psum((gain_terms, kernel_local), ('fsdp', 'ctx'))  59 us
    convert_element_type x1, other arithmetic, attend_back(): score_grad = (probs * (probs_grad - center)).astype(jnp.bfloat16)  52.7 us
    dot_general x1, matrix products, attend_back(): jnp.einsum('fhe,lhe->hfl', mixed_grad, values, preferred_element_type=jnp...  45 us
    psum x1, blocking collectives, per_device(): lax.psum((jnp.sum(shifted_grad, (0, 1)), jnp.sum(shifted_grad * unit, (0,...  33 us
    psum x1, blocking collectives, per_device(): lax.psum((jnp.sum(live_cube * filtered, (0, 1)), jnp.sum(live_cube * filt...  32 us
    reduce_scatter x1, waiting for transfers between devices, per_device(): lax.psum_scatter(weight_grads[0].astype(jnp.bfloat16), 'fsdp', scatter_di...  29.1 us
    all_gather x1, waiting for transfers between devices, per_device(): lax.all_gather(feed_up, 'fsdp', axis=0, tiled=True)  28.7 us
  transfers between devices with their start and end apart: 27, of which 23 were waited for; matrix products, arithmetic and copies ran while one was open for 8% of the time, Pallas kernels for 0%

profile of v1, /device:TPU:0, one launch (start us, length us, event | category | flops | bytes accessed | tf_op | source)
XLA Modules:
  0.0 1161.4 jit_solution(15022702373127900767)
XLA Ops:
  11.6 28.7 %all-gather.22.cloned.1.call-done = bf16[512,1024]{1,0:T(8,128)(2,1)} async-done(((bf16[128,1024]{1,0:T(8,128)(2,1)}), bf16[512,1024]{1,0:T(8,128)(2,1)}) %all-gather.22.cloned.1.call-update) | async-done | bytes 1048592 | tf_op jit(solution)/shard_map/all_gather | solution.py:159
  40.3 5.1 multiply_convert_fusion.2
  45.4 23.9 %all-gather.24.cloned.1.call-done = bf16[512,1024]{1,0:T(8,128)(2,1)} async-done(((bf16[128,1024]{1,0:T(8,128)(2,1)}), bf16[512,1024]{1,0:T(8,128)(2,1)}) %all-gather.24.cloned.1.call-update) | async-done | bytes 1048592 | tf_op jit(solution)/shard_map/all_gather | solution.py:160
  69.3 4.1 convolution_convert_fusion.10
  73.5 18.0 %all_gather.79 = bf16[512,3,256]{2,0,1:T(8,128)(2,1)S(1)} all-gather(bf16[128,3,256]{2,0,1:T(8,128)(2,1)S(1)} %copy-done.74), channel_id=1, replica_groups=mesh['fsdp'=4,'ctx'=4,'tp'=2] {'fsdp'}, dimensions={0}, use_global_device_ids=true | all-gather | bytes 983040 | tf_op jit(solution)/shard_map/all_gather | solution.py:161
  93.3 12.8 %all-gather.32.cloned.1.call-done = bf16[2048,512]{1,0:T(8,128)(2,1)} async-done(((bf16[1024,512]{1,0:T(8,128)(2,1)}), bf16[2048,512]{1,0:T(8,128)(2,1)}) %all-gather.32.cloned.1.call-update) | async-done | bytes 2097168 | tf_op jit(solution)/shard_map/all_gather | solution.py:51
  106.1 2.6 reduce_sum.727
  114.5 14.0 %all_gather.81 = bf16[512,256]{1,0:T(8,128)(2,1)S(1)} all-gather(bf16[128,256]{1,0:T(8,128)(2,1)S(1)} %copy-done.100), channel_id=1, replica_groups=mesh['fsdp'=4,'ctx'=4,'tp'=2] {'fsdp'}, dimensions={0}, use_global_device_ids=true | all-gather | bytes 327680 | tf_op jit(solution)/shard_map/all_gather | solution.py:162
  128.6 19.9 %all-gather.26.cloned.1.call-done = bf16[1,4096,512]{1,2,0:T(8,128)(2,1)} async-done(((bf16[1,1024,512]{1,2,0:T(8,128)(2,1)}), bf16[1,4096,512]{1,2,0:T(8,128)(2,1)}) %all-gather.26.cloned.1.call-update) | async-done | bytes 4194320 | tf_op jit(solution)/shard_map/all_gather | solution.py:192
  148.4 4.0 fusion.282
  152.4 23.2 %select_reduce_fusion = (f32[4,1024]{1,0:T(4,128)S(1)}, f32[4,1024,4096]{2,1,0:T(8,128)}) fusion(pred[4096]{0:T(1024)(128)(4,1)S(1)} %iota_compare_fusion, bf16[4096,4,64]{0,2,1:T(8,128)(2,1)S(1)} %bitcast.334, f32[1024,4,32]{0,2,1:T(8,128)S(1)} %get-tuple-element.158, f32[1024,4,32]{0,2,1:T(8,128)S(1)} %get-tuple-element.157), kind=kOutput, calls=%fused_computation.6 | convolution fusion | flops 2181820416 | bytes 70275072 | tf_op jit(solution)/shard_map/while/body/eval_jaxpr/fhe,lhe->hfl/dot_general | solution.py:99
  175.6 21.4 %fusion = f32[4,1024]{1,0:T(4,128)S(1)} fusion(f32[4,1024,4096]{2,1,0:T(8,128)} %get-tuple-element.216, f32[4,1024]{1,0:T(4,128)S(1)} %get-tuple-element.215, pred[4096]{0:T(1024)(128)(4,1)S(1)} %iota_compare_fusion), kind=kLoop, calls=%fused_computation.5 | loop fusion | flops 50327552 | bytes 67145728 | tf_op jit(solution)/shard_map/while/body/eval_jaxpr/reduce_sum | solution.py:110
  197.0 23.9 %fusion.55 = bf16[4,64,1024]{2,1,0:T(8,128)(2,1)S(1)} fusion(bf16[4096,4,64]{0,2,1:T(8,128)(2,1)S(1)} %bitcast.340, f32[4,1024,4096]{2,1,0:T(8,128)} %get-tuple-element.216, f32[4,1024]{1,0:T(4,128)S(1)} %fusion, f32[4,1024]{1,0:T(4,128)S(1)} %get-tuple-element.215, pred[4096]{0:T(1024)(128)(4,1)S(1)} %iota_compare_fusion), kind=kOutput, calls=%fused_computation.258 | convolution fusion | flops 2214854656 | bytes 69767168 | tf_op jit(solution)/shard_map/while/body/eval_jaxpr/hfl,lhe->fhe/dot_general | solution.py:112
  222.7 16.5 %all_gather.84 = bf16[512,2,256]{2,0,1:T(8,128)(2,1)} all-gather(bf16[128,2,256]{2,0,1:T(8,128)(2,1)S(1)} %copy.28), channel_id=1, replica_groups=mesh['fsdp'=4,'ctx'=4,'tp'=2] {'fsdp'}, dimensions={0}, use_global_device_ids=true | all-gather | bytes 655360 | tf_op jit(solution)/shard_map/all_gather | solution.py:163
  240.5 15.3 %all-gather.34.cloned.1.call-done = bf16[2048,512]{1,0:T(8,128)(2,1)} async-done(((bf16[1024,512]{1,0:T(8,128)(2,1)}), bf16[2048,512]{1,0:T(8,128)(2,1)}) %all-gather.34.cloned.1.call-update) | async-done | bytes 2097168 | tf_op jit(solution)/shard_map/all_gather | solution.py:51
  255.8 2.6 reduce_sum.731
  265.9 14.7 %all_gather.85 = bf16[512,256]{1,0:T(8,128)(2,1)S(1)} all-gather(bf16[128,256]{1,0:T(8,128)(2,1)S(1)} %copy-done.101), channel_id=1, replica_groups=mesh['fsdp'=4,'ctx'=4,'tp'=2] {'fsdp'}, dimensions={0}, use_global_device_ids=true | all-gather | bytes 327680 | tf_op jit(solution)/shard_map/all_gather | solution.py:164
  281.5 8.0 fusion.86
  289.5 32.0 %all-reduce.8 = (f32[256]{0:T(256)S(1)}, f32[]{:T(128)}, f32[256]{0:T(256)S(1)}) all-reduce(f32[256]{0:T(256)S(1)} %get-tuple-element.109, f32[]{:T(128)} %fusion.247, f32[256]{0:T(256)S(1)} %get-tuple-element.108), channel_id=1, replica_groups=mesh['fsdp'=4,'ctx'=4,'tp'=2] {'fsdp','ctx'}, use_global_device_ids=true, to_apply=%region_11.12 | all-reduce | flops 513 | bytes 4104 | tf_op jit(solution)/shard_map/psum | solution.py:213
  325.8 28.0 %all-gather.36.cloned.1.call-done = bf16[2048,512]{1,0:T(8,128)(2,1)} async-done(((bf16[1024,512]{1,0:T(8,128)(2,1)}), bf16[2048,512]{1,0:T(8,128)(2,1)}) %all-gather.36.cloned.1.call-update) | async-done | bytes 2097168 | tf_op jit(solution)/shard_map/all_gather | solution.py:51
  353.8 2.6 reduce_sum.737
  359.2 24.2 %all-gather.28.cloned.1.call-done = bf16[512,1024]{1,0:T(8,128)(2,1)} async-done(((bf16[128,1024]{1,0:T(8,128)(2,1)}), bf16[512,1024]{1,0:T(8,128)(2,1)}) %all-gather.28.cloned.1.call-update) | async-done | bytes 1048592 | tf_op jit(solution)/shard_map/all_gather | solution.py:165
  383.4 5.0 multiply_convert_fusion.1
  388.5 23.9 %all-gather.30.cloned.1.call-done = bf16[512,1024]{1,0:T(8,128)(2,1)} async-done(((bf16[128,1024]{1,0:T(8,128)(2,1)}), bf16[512,1024]{1,0:T(8,128)(2,1)}) %all-gather.30.cloned.1.call-update) | async-done | bytes 1048592 | tf_op jit(solution)/shard_map/all_gather | solution.py:166
  412.4 4.1 convolution_convert_fusion.7
  417.0 32.2 %all-gather.38.cloned.1.call-done = bf16[2048,512]{1,0:T(8,128)(2,1)} async-done(((bf16[1024,512]{1,0:T(8,128)(2,1)}), bf16[2048,512]{1,0:T(8,128)(2,1)}) %all-gather.38.cloned.1.call-update) | async-done | bytes 2097168 | tf_op jit(solution)/shard_map/all_gather | solution.py:51
  449.1 2.6 reduce_sum.740
  464.7 33.2 %all-gather.40.cloned.1.call-done = bf16[2048,512]{1,0:T(8,128)(2,1)} async-done(((bf16[1024,512]{1,0:T(8,128)(2,1)}), bf16[2048,512]{1,0:T(8,128)(2,1)}) %all-gather.40.cloned.1.call-update) | async-done | bytes 2097168 | tf_op jit(solution)/shard_map/all_gather | solution.py:51
  497.9 2.6 reduce_sum.745
  507.8 33.0 %all-reduce.7 = (f32[256]{0:T(256)S(1)}, f32[256]{0:T(256)S(1)}) all-reduce(f32[256]{0:T(256)S(1)} %get-tuple-element.219, f32[256]{0:T(256)S(1)} %reduce_sum.748), channel_id=1, replica_groups=mesh['fsdp'=4,'ctx'=4,'tp'=2] {'fsdp','ctx'}, use_global_device_ids=true, to_apply=%region_30.31 | all-reduce | flops 512 | bytes 4096 | tf_op jit(solution)/shard_map/psum | solution.py:243
  541.5 5.4 fusion.140
  548.3 3.2 collective-permute-start.3
  552.3 8.5 fusion.89
  564.1 31.1 %all-gather.42.cloned.1.call-done = bf16[2048,512]{1,0:T(8,128)(2,1)} async-done(((bf16[1024,512]{1,0:T(8,128)(2,1)}), bf16[2048,512]{1,0:T(8,128)(2,1)}) %all-gather.42.cloned.1.call-update) | async-done | bytes 2097168 | tf_op jit(solution)/shard_map/all_gather | solution.py:51
  595.2 2.6 reduce_sum.750
  601.6 24.1 %fusion.6 = bf16[4,64,4096]{2,1,0:T(8,128)(2,1)S(1)} fusion(bf16[1024,4,64]{0,2,1:T(8,128)(2,1)S(1)} %bitcast.338, f32[4,1024,4096]{2,1,0:T(8,128)} %get-tuple-element.216, f32[4,1024]{1,0:T(4,128)S(1)} %log_add_fusion, pred[4096]{0:T(1024)(128)(4,1)S(1)} %iota_compare_fusion), kind=kOutput, calls=%fused_computation.45 | convolution fusion | flops 2198863872 | bytes 69750784 | tf_op jit(solution)/shard_map/while/body/eval_jaxpr/hfl,fhe->lhe/dot_general | solution.py:126
  625.7 45.0 %multiply_reduce_fusion = (f32[4,1024]{1,0:T(4,128)S(1)}, f32[4,1024,4096]{2,1,0:T(8,128)}) fusion(f32[4,1024,4096]{2,1,0:T(8,128)} %get-tuple-element.216, f32[4,1024]{1,0:T(4,128)S(1)} %log_add_fusion, pred[4096]{0:T(1024)(128)(4,1)S(1)} %iota_compare_fusion, bf16[1024,4,64]{0,2,1:T(8,128)(2,1)S(1)} %bitcast.339, bf16[4096,4,64]{0,2,1:T(8,128)(2,1)S(1)} %bitcast.341), kind=kOutput, calls=%fused_computation.1 | convolution fusion | flops 2214588416 | bytes 136876032 | tf_op jit(solution)/shard_map/while/body/eval_jaxpr/fhe,lhe->hfl/dot_general | solution.py:121
  673.2 52.7 %multiply_convert_fusion = bf16[4,1024,4096]{2,1,0:T(8,128)(2,1)} fusion(f32[4,1024,4096]{2,1,0:T(8,128)} %get-tuple-element.222, f32[4,1024,4096]{2,1,0:T(8,128)} %get-tuple-element.216, f32[4,1024]{1,0:T(4,128)S(1)} %get-tuple-element.221, f32[4,1024]{1,0:T(4,128)S(1)} %log_add_fusion, pred[4096]{0:T(1024)(128)(4,1)S(1)} %iota_compare_fusion), kind=kLoop, calls=%fused_computation | loop fusion | flops 83886080 | bytes 167809024 | tf_op jit(solution)/shard_map/while/body/eval_jaxpr/convert_element_type | solution.py:123
  726.0 13.8 %convolution_convert_fusion = bf16[4,64,4096]{2,1,0:T(8,128)(2,1)S(1)} fusion(bf16[4,1024,4096]{2,1,0:T(8,128)(2,1)} %multiply_convert_fusion, f32[1024,4,32]{0,2,1:T(8,128)S(1)} %copy-done.45, f32[1024,4,32]{0,2,1:T(8,128)S(1)} %copy-done.43), kind=kOutput, calls=%fused_computation.46 | convolution fusion | flops 2149318656 | bytes 36700160 | tf_op jit(solution)/shard_map/while/body/eval_jaxpr/hfl,fhe->lhe/dot_general | solution.py:125
  742.3 4.5 pad_maximum_fusion
  748.4 17.2 %fusion.54 = f32[1,1024,4,64]{1,3,2,0:T(8,128)S(1)} fusion(bf16[4096,4,64]{0,2,1:T(8,128)(2,1)S(1)} %bitcast.335, bf16[4,1024,4096]{2,1,0:T(8,128)(2,1)} %multiply_convert_fusion), kind=kOutput, calls=%fused_computation.224 | convolution fusion | flops 2147745792 | bytes 36700160 | tf_op jit(solution)/shard_map/while/body/eval_jaxpr/hfl,lhe->fhe/dot_general | solution.py:124
  765.6 25.9 %reduce-scatter.10.cloned.1.call-done = bf16[1,1024,512]{2,1,0:T(8,128)(2,1)} async-done(((bf16[1,4096,512]{2,1,0:T(8,128)(2,1)}), bf16[1,1024,512]{2,1,0:T(8,128)(2,1)}) %reduce-scatter.10.cloned.1.call-update) | async-done | bytes 1048592 | tf_op jit(solution)/shard_map/reduce_scatter | solution.py:285
  797.7 33.2 %all-gather.44.cloned.1.call-done = bf16[2048,512]{1,0:T(8,128)(2,1)} async-done(((bf16[1024,512]{1,0:T(8,128)(2,1)}), bf16[2048,512]{1,0:T(8,128)(2,1)}) %all-gather.44.cloned.1.call-update) | async-done | bytes 2097168 | tf_op jit(solution)/shard_map/all_gather | solution.py:51
  830.9 2.6 reduce_sum.754
  845.1 4.0 convolution_convert_fusion.2
  849.4 5.0 convolution_convert_fusion.1
  854.5 3.2 convolution_convert_fusion.13
  857.8 4.2 convolution_convert_fusion.11
  862.1 4.0 convolution_convert_fusion.4
  866.3 3.9 convolution_convert_fusion.3
  870.2 8.0 all-gather.46.cloned.1.call-done
  878.2 2.6 reduce_sum.757
  882.6 2.7 fusion.50
  885.5 8.6 fusion.36
  895.4 4.2 multiply_multiply_fusion
  903.6 4.1 reduce-scatter.24.cloned.1.call-done
  907.7 28.0 %reduce-scatter.26.cloned.1.call-done = bf16[128,1024]{1,0:T(8,128)(2,1)} async-done(((bf16[512,1024]{1,0:T(8,128)(2,1)}), bf16[128,1024]{1,0:T(8,128)(2,1)}) %reduce-scatter.26.cloned.1.call-update) | async-done | bytes 262160 | tf_op jit(solution)/shard_map/reduce_scatter | solution.py:342
  935.7 23.1 %reduce-scatter.20.cloned.1.call-done = bf16[128,2,256]{2,0,1:T(8,128)(2,1)} async-done(((bf16[512,2,256]{2,0,1:T(8,128)(2,1)}), bf16[128,2,256]{2,0,1:T(8,128)(2,1)}) %reduce-scatter.20.cloned.1.call-update) | async-done | bytes 131088 | tf_op jit(solution)/shard_map/reduce_scatter | solution.py:333
  958.7 23.6 %reduce-scatter.16.cloned.1.call-done = bf16[128,3,256]{2,0,1:T(8,128)(2,1)} async-done(((bf16[512,3,256]{2,0,1:T(8,128)(2,1)}), bf16[128,3,256]{2,0,1:T(8,128)(2,1)}) %reduce-scatter.16.cloned.1.call-update) | async-done | bytes 196624 | tf_op jit(solution)/shard_map/reduce_scatter | solution.py:327
  982.3 29.1 %reduce-scatter.12.cloned.1.call-done = bf16[128,1024]{1,0:T(8,128)(2,1)} async-done(((bf16[512,1024]{1,0:T(8,128)(2,1)}), bf16[128,1024]{1,0:T(8,128)(2,1)}) %reduce-scatter.12.cloned.1.call-update) | async-done | bytes 262160 | tf_op jit(solution)/shard_map/reduce_scatter | solution.py:321
  1011.4 27.9 %reduce-scatter.14.cloned.1.call-done = bf16[128,1024]{1,0:T(8,128)(2,1)} async-done(((bf16[512,1024]{1,0:T(8,128)(2,1)}), bf16[128,1024]{1,0:T(8,128)(2,1)}) %reduce-scatter.14.cloned.1.call-update) | async-done | bytes 262160 | tf_op jit(solution)/shard_map/reduce_scatter | solution.py:324
  1039.4 21.3 %reduce-scatter.18.cloned.1.call-done = bf16[128,256]{1,0:T(8,128)(2,1)} async-done(((bf16[512,256]{1,0:T(8,128)(2,1)}), bf16[128,256]{1,0:T(8,128)(2,1)}) %reduce-scatter.18.cloned.1.call-update) | async-done | bytes 65552 | tf_op jit(solution)/shard_map/reduce_scatter | solution.py:330
  1060.7 21.1 %reduce-scatter.22.cloned.1.call-done = bf16[128,256]{1,0:T(8,128)(2,1)} async-done(((bf16[512,256]{1,0:T(8,128)(2,1)}), bf16[128,256]{1,0:T(8,128)(2,1)}) %reduce-scatter.22.cloned.1.call-update) | async-done | bytes 65552 | tf_op jit(solution)/shard_map/reduce_scatter | solution.py:336
  1084.8 59.0 %all-reduce.6 = (f32[5,512]{1,0:T(8,128)}, f32[31,256]{1,0:T(8,128)}) all-reduce(f32[5,512]{1,0:T(8,128)S(1)} %stack.128, f32[31,256]{1,0:T(8,128)S(1)} %stack.160), channel_id=1, replica_groups=mesh['fsdp'=4,'ctx'=4,'tp'=2] {'fsdp','ctx'}, use_global_device_ids=true, to_apply=%region_47.48 | all-reduce | flops 10496 | bytes 83968 | tf_op jit(solution)/shard_map/psum | solution.py:309
  (557 shorter events, 103.6 us)
Async XLA Ops:
  7.2 33.1 %all-gather.22.cloned.1.call-start = ((), (), s32[]{:S(2)}) async-start(), calls=%async_computation.9 | async-start | bytes 1310720 | tf_op jit(solution)/shard_map/all_gather | solution.py:159
  7.9 61.3 %all-gather.24.cloned.1.call-start = ((), (), s32[]{:S(2)}) async-start(), calls=%async_computation.10 | async-start | bytes 1310720 | tf_op jit(solution)/shard_map/all_gather | solution.py:160
  8.7 97.4 %all-gather.32.cloned.1.call-start = ((), (), s32[]{:S(2)}) async-start(), calls=%async_computation.23 | async-start | bytes 3145728 | tf_op jit(solution)/shard_map/all_gather | solution.py:51
  11.6 97.9 %copy-start.104 = (f32[1,512]{1,0:T(1,128)}, f32[1,512]{1,0:T(1,128)S(1)}, u32[]{:S(2)}) copy-start(f32[1,512]{1,0:T(1,128)S(1)} %get-tuple-element.204) | copy-start | bytes 6148
  11.6 587.6 %copy-start.102 = (f32[1,512]{1,0:T(1,128)}, f32[1,512]{1,0:T(1,128)S(1)}, u32[]{:S(2)}) copy-start(f32[1,512]{1,0:T(1,128)S(1)} %get-tuple-element.203) | copy-start | bytes 6148
  73.4 75.0 %all-gather.26.cloned.1.call-start = ((), (), s32[]{:S(2)}) async-start(), calls=%async_computation.11 | async-start | bytes 5242880 | tf_op jit(solution)/shard_map/all_gather | solution.py:192
  113.8 142.0 %all-gather.34.cloned.1.call-start = ((), (), s32[]{:S(2)}) async-start(), calls=%async_computation.24 | async-start | bytes 3145728 | tf_op jit(solution)/shard_map/all_gather | solution.py:51
  222.6 131.3 %all-gather.36.cloned.1.call-start = ((), (), s32[]{:S(2)}) async-start(), calls=%async_computation.25 | async-start | bytes 3145728 | tf_op jit(solution)/shard_map/all_gather | solution.py:51
  239.8 301.1 %copy-start.127 = (f32[1,256]{1,0:T(1,128)}, f32[1,256]{1,0:T(1,128)S(1)}, u32[]{:S(2)}) copy-start(f32[1,256]{1,0:T(1,128)S(1)} %get-tuple-element.211) | copy-start | bytes 3076
  259.4 339.8 %copy-start.81 = (f32[1024]{0:T(1024)}, f32[1024]{0:T(1024)S(1)}, u32[]{:S(2)}) copy-start(f32[1024]{0:T(1024)S(1)} %broadcast_multiply_fusion.2) | copy-start | bytes 12292
  259.9 339.4 %copy-start.92 = (f32[1024]{0:T(1024)}, f32[1024]{0:T(1024)S(1)}, u32[]{:S(2)}) copy-start(f32[1024]{0:T(1024)S(1)} %fusion.244) | copy-start | bytes 12292
  261.8 60.9 %copy-start.189 = (f32[1,256]{1,0:T(1,128)S(1)}, f32[1,256]{1,0:T(1,128)}, u32[]{:S(2)}) copy-start(f32[1,256]{1,0:T(1,128)} %get-tuple-element.212) | copy-start | bytes 3076
  263.0 18.2 %collective-permute-start = (bf16[1,15,256]{2,1,0:T(8,128)(2,1)S(1)}, bf16[1,15,256]{2,1,0:T(8,128)(2,1)S(1)}, u32[]{:S(2)}, u32[]{:S(2)}) collective-permute-start(bf16[1,15,256]{2,1,0:T(8,128)(2,1)S(1)} %get-tuple-element.165), channel_id=1, source_target_pairs={{0,2},{2,4},{4,6},{1,3},{3,5},{5,7},{8,10},{10,12},{12,14},{9,11},... | collective-permute-start | bytes 23048 | tf_op jit(solution)/shard_map/ppermute | solution.py:20
  264.6 16.7 %collective-permute-start.1 = (bf16[1,15,256]{2,1,0:T(8,128)(2,1)S(1)}, bf16[1,15,256]{2,1,0:T(8,128)(2,1)S(1)}, u32[]{:S(2)}, u32[]{:S(2)}) collective-permute-start(bf16[1,15,256]{2,1,0:T(8,128)(2,1)S(1)} %get-tuple-element.166), channel_id=1, source_target_pairs={{2,0},{4,2},{6,4},{3,1},{5,3},{7,5},{10,8},{12,10},{14,12},{11,9},... | collective-permute-start | bytes 23048 | tf_op jit(solution)/shard_map/ppermute | solution.py:22
  281.3 260.3 %copy-start.83 = (bf16[1,15,256]{2,1,0:T(8,128)(2,1)}, bf16[1,15,256]{2,1,0:T(8,128)(2,1)S(1)}, u32[]{:S(2)}) copy-start(bf16[1,15,256]{2,1,0:T(8,128)(2,1)S(1)} %collective-permute-done.1) | copy-start | bytes 23044
  324.3 59.1 %all-gather.28.cloned.1.call-start = ((), (), s32[]{:S(2)}) async-start(), calls=%async_computation.12 | async-start | bytes 1310720 | tf_op jit(solution)/shard_map/all_gather | solution.py:165
  325.0 87.4 %all-gather.30.cloned.1.call-start = ((), (), s32[]{:S(2)}) async-start(), calls=%async_computation.13 | async-start | bytes 1310720 | tf_op jit(solution)/shard_map/all_gather | solution.py:166
  325.8 123.4 %all-gather.38.cloned.1.call-start = ((), (), s32[]{:S(2)}) async-start(), calls=%async_computation.26 | async-start | bytes 3145728 | tf_op jit(solution)/shard_map/all_gather | solution.py:51
  358.7 144.3 %copy-start = (f32[1024,512]{1,0:T(8,128)}, f32[1024,512]{1,0:T(8,128)S(1)}, u32[]{:S(2)}) copy-start(f32[1024,512]{1,0:T(8,128)S(1)} %get-tuple-element.143) | copy-start | bytes 6291460
  358.8 144.3 %copy-start.79 = (f32[1024]{0:T(1024)}, f32[1024]{0:T(1024)S(1)}, u32[]{:S(2)}) copy-start(f32[1024]{0:T(1024)S(1)} %broadcast_multiply_fusion.1) | copy-start | bytes 12292
  359.2 143.8 %copy-start.98 = (f32[1024]{0:T(1024)}, f32[1024]{0:T(1024)S(1)}, u32[]{:S(2)}) copy-start(f32[1024]{0:T(1024)S(1)} %fusion.245) | copy-start | bytes 12292
  416.5 81.4 %all-gather.40.cloned.1.call-start = ((), (), s32[]{:S(2)}) async-start(), calls=%async_computation.27 | async-start | bytes 3145728 | tf_op jit(solution)/shard_map/all_gather | solution.py:51
  456.5 46.5 %copy-start.116 = (f32[1024]{0:T(1024)}, f32[1024]{0:T(1024)S(1)}, u32[]{:S(2)}) copy-start(f32[1024]{0:T(1024)S(1)} %negate_multiply_fusion.4) | copy-start | bytes 12292
  464.6 130.6 %all-gather.42.cloned.1.call-start = ((), (), s32[]{:S(2)}) async-start(), calls=%async_computation.28 | async-start | bytes 3145728 | tf_op jit(solution)/shard_map/all_gather | solution.py:51
  506.2 46.0 %copy-start.22 = (f32[1024,2,256]{2,0,1:T(8,128)S(1)}, f32[1024,2,256]{2,0,1:T(8,128)}, u32[]{:S(2)}) copy-start(f32[1024,2,256]{2,0,1:T(8,128)} %copy-done.21) | copy-start | bytes 6291460
  506.2 46.0 %copy-start.130 = (f32[1,256]{1,0:T(1,128)S(1)}, f32[1,256]{1,0:T(1,128)}, u32[]{:S(2)}) copy-start(f32[1,256]{1,0:T(1,128)} %copy-done.129) | copy-start | bytes 3076
  506.2 46.0 %copy-start.132 = (f32[1,256]{1,0:T(1,128)S(1)}, f32[1,256]{1,0:T(1,128)}, u32[]{:S(2)}) copy-start(f32[1,256]{1,0:T(1,128)} %copy-done.131) | copy-start | bytes 3076
  506.2 46.0 %copy-start.134 = (f32[1,256]{1,0:T(1,128)S(1)}, f32[1,256]{1,0:T(1,128)}, u32[]{:S(2)}) copy-start(f32[1,256]{1,0:T(1,128)} %copy-done.133) | copy-start | bytes 3076
  506.2 46.0 %copy-start.136 = (f32[1,256]{1,0:T(1,128)S(1)}, f32[1,256]{1,0:T(1,128)}, u32[]{:S(2)}) copy-start(f32[1,256]{1,0:T(1,128)} %copy-done.135) | copy-start | bytes 3076
  506.2 46.0 %copy-start.138 = (f32[1,256]{1,0:T(1,128)S(1)}, f32[1,256]{1,0:T(1,128)}, u32[]{:S(2)}) copy-start(f32[1,256]{1,0:T(1,128)} %get-tuple-element.176) | copy-start | bytes 3076
  506.2 46.0 %copy-start.140 = (f32[1,256]{1,0:T(1,128)S(1)}, f32[1,256]{1,0:T(1,128)}, u32[]{:S(2)}) copy-start(f32[1,256]{1,0:T(1,128)} %get-tuple-element.177) | copy-start | bytes 3076
  506.2 46.0 %copy-start.142 = (f32[1,256]{1,0:T(1,128)S(1)}, f32[1,256]{1,0:T(1,128)}, u32[]{:S(2)}) copy-start(f32[1,256]{1,0:T(1,128)} %get-tuple-element.178) | copy-start | bytes 3076
  506.2 46.0 %copy-start.144 = (f32[1,256]{1,0:T(1,128)S(1)}, f32[1,256]{1,0:T(1,128)}, u32[]{:S(2)}) copy-start(f32[1,256]{1,0:T(1,128)} %get-tuple-element.179) | copy-start | bytes 3076
  506.2 46.0 %copy-start.146 = (f32[1,256]{1,0:T(1,128)S(1)}, f32[1,256]{1,0:T(1,128)}, u32[]{:S(2)}) copy-start(f32[1,256]{1,0:T(1,128)} %get-tuple-element.180) | copy-start | bytes 3076
  506.3 46.0 %copy-start.148 = (f32[1,256]{1,0:T(1,128)S(1)}, f32[1,256]{1,0:T(1,128)}, u32[]{:S(2)}) copy-start(f32[1,256]{1,0:T(1,128)} %get-tuple-element.181) | copy-start | bytes 3076
  506.3 46.0 %copy-start.150 = (f32[1,256]{1,0:T(1,128)S(1)}, f32[1,256]{1,0:T(1,128)}, u32[]{:S(2)}) copy-start(f32[1,256]{1,0:T(1,128)} %get-tuple-element.182) | copy-start | bytes 3076
  506.3 46.0 %copy-start.152 = (f32[1,256]{1,0:T(1,128)S(1)}, f32[1,256]{1,0:T(1,128)}, u32[]{:S(2)}) copy-start(f32[1,256]{1,0:T(1,128)} %get-tuple-element.183) | copy-start | bytes 3076
  547.0 4.5 collective-permute-start.2
  548.3 3.8 collective-permute-start.3
  564.1 227.5 %reduce-scatter.10.cloned.1.call-start = ((), (), s32[]{:S(2)}) async-start(), calls=%async_computation.14 | async-start | bytes 5242880 | tf_op jit(solution)/shard_map/reduce_scatter | solution.py:285
  673.2 52.7 %copy-start.43 = (f32[1024,4,32]{0,2,1:T(8,128)S(1)}, f32[1024,4,32]{0,2,1:T(8,128)}, u32[]{:S(2)}) copy-start(f32[1024,4,32]{0,2,1:T(8,128)} %copy-done.42) | copy-start | bytes 1572868
  673.2 52.7 %copy-start.45 = (f32[1024,4,32]{0,2,1:T(8,128)S(1)}, f32[1024,4,32]{0,2,1:T(8,128)}, u32[]{:S(2)}) copy-start(f32[1024,4,32]{0,2,1:T(8,128)} %copy-done.44) | copy-start | bytes 1572868
  746.8 84.1 %all-gather.44.cloned.1.call-start = ((), (), s32[]{:S(2)}) async-start(), calls=%async_computation.29 | async-start | bytes 3145728 | tf_op jit(solution)/shard_map/all_gather | solution.py:51
  797.7 80.5 %all-gather.46.cloned.1.call-start = ((), (), s32[]{:S(2)}) async-start(), calls=%async_computation.30 | async-start | bytes 3145728 | tf_op jit(solution)/shard_map/all_gather | solution.py:51
  845.0 62.7 %reduce-scatter.24.cloned.1.call-start = ((), (), s32[]{:S(2)}) async-start(), calls=%async_computation.21 | async-start | bytes 1310720 | tf_op jit(solution)/shard_map/reduce_scatter | solution.py:339
  849.1 86.5 %reduce-scatter.26.cloned.1.call-start = ((), (), s32[]{:S(2)}) async-start(), calls=%async_computation.22 | async-start | bytes 1310720 | tf_op jit(solution)/shard_map/reduce_scatter | solution.py:342
  854.4 104.3 %reduce-scatter.20.cloned.1.call-start = ((), (), s32[]{:S(2)}) async-start(), calls=%async_computation.19 | async-start | bytes 655360 | tf_op jit(solution)/shard_map/reduce_scatter | solution.py:333
  857.7 124.6 %reduce-scatter.16.cloned.1.call-start = ((), (), s32[]{:S(2)}) async-start(), calls=%async_computation.17 | async-start | bytes 983040 | tf_op jit(solution)/shard_map/reduce_scatter | solution.py:327
  862.0 149.4 %reduce-scatter.12.cloned.1.call-start = ((), (), s32[]{:S(2)}) async-start(), calls=%async_computation.15 | async-start | bytes 1310720 | tf_op jit(solution)/shard_map/reduce_scatter | solution.py:321
  866.2 173.2 %reduce-scatter.14.cloned.1.call-start = ((), (), s32[]{:S(2)}) async-start(), calls=%async_computation.16 | async-start | bytes 1310720 | tf_op jit(solution)/shard_map/reduce_scatter | solution.py:324
  870.2 190.6 %reduce-scatter.18.cloned.1.call-start = ((), (), s32[]{:S(2)}) async-start(), calls=%async_computation.18 | async-start | bytes 327680 | tf_op jit(solution)/shard_map/reduce_scatter | solution.py:330
  895.3 186.5 %reduce-scatter.22.cloned.1.call-start = ((), (), s32[]{:S(2)}) async-start(), calls=%async_computation.20 | async-start | bytes 327680 | tf_op jit(solution)/shard_map/reduce_scatter | solution.py:336
  901.1 242.7 %all-reduce.12.cloned.1.call-start = ((), (), s32[]{:S(2)}) async-start(), calls=%async_computation.31 | async-start | bytes 3014656 | tf_op jit(solution)/shard_map/psum | solution.py:351
  903.5 180.6 %copy-start.169 = (f32[256]{0:T(256)S(1)}, f32[256]{0:T(256)}, u32[]{:S(2)}) copy-start(f32[256]{0:T(256)} %get-tuple-element.84) | copy-start | bytes 3076
  903.5 180.6 %copy-start.170 = (f32[256]{0:T(256)S(1)}, f32[256]{0:T(256)}, u32[]{:S(2)}) copy-start(f32[256]{0:T(256)} %get-tuple-element.85) | copy-start | bytes 3076
  903.5 180.6 %copy-start.171 = (f32[256]{0:T(256)S(1)}, f32[256]{0:T(256)}, u32[]{:S(2)}) copy-start(f32[256]{0:T(256)} %get-tuple-element.86) | copy-start | bytes 3076
  903.5 180.6 %copy-start.172 = (f32[256]{0:T(256)S(1)}, f32[256]{0:T(256)}, u32[]{:S(2)}) copy-start(f32[256]{0:T(256)} %get-tuple-element.87) | copy-start | bytes 3076
  903.5 180.6 %copy-start.173 = (f32[256]{0:T(256)S(1)}, f32[256]{0:T(256)}, u32[]{:S(2)}) copy-start(f32[256]{0:T(256)} %get-tuple-element.88) | copy-start | bytes 3076
  903.5 180.6 %copy-start.174 = (f32[256]{0:T(256)S(1)}, f32[256]{0:T(256)}, u32[]{:S(2)}) copy-start(f32[256]{0:T(256)} %get-tuple-element.89) | copy-start | bytes 3076
  903.5 180.7 %copy-start.177 = (f32[256]{0:T(256)S(1)}, f32[256]{0:T(256)}, u32[]{:S(2)}) copy-start(f32[256]{0:T(256)} %copy-done.176) | copy-start | bytes 3076
  903.5 180.7 %copy-start.179 = (f32[256]{0:T(256)S(1)}, f32[256]{0:T(256)}, u32[]{:S(2)}) copy-start(f32[256]{0:T(256)} %copy-done.178) | copy-start | bytes 3076
  903.6 181.2 %copy-start.165 = (f32[512]{0:T(512)S(1)}, f32[512]{0:T(512)}, u32[]{:S(2)}) copy-start(f32[512]{0:T(512)} %get-tuple-element.68) | copy-start | bytes 6148
  903.6 181.2 %copy-start.166 = (f32[512]{0:T(512)S(1)}, f32[512]{0:T(512)}, u32[]{:S(2)}) copy-start(f32[512]{0:T(512)} %get-tuple-element.70) | copy-start | bytes 6148
  903.6 181.2 %copy-start.167 = (f32[512]{0:T(512)S(1)}, f32[512]{0:T(512)}, u32[]{:S(2)}) copy-start(f32[512]{0:T(512)} %get-tuple-element.76) | copy-start | bytes 6148
  (163 other events, 1990.9 us)
Sparse Core Ops, SparseCore 0:
  9.6 30.6 all-gather.21
  41.9 27.3 all-gather.23
  73.6 32.4 all-gather.31
  113.9 34.4 all-gather.25
  222.7 33.0 all-gather.33
  324.4 29.4 all-gather.35
  355.4 27.9 all-gather.27
  385.0 27.3 all-gather.29
  416.6 32.4 all-gather.37
  464.7 33.0 all-gather.39
  564.2 30.9 all-gather.41
  746.9 44.5 reduce-scatter.9
  797.8 33.0 all-gather.43
  845.1 33.0 all-gather.45
  880.4 27.2 reduce-scatter.23
  909.8 25.7 reduce-scatter.25
  938.4 20.3 reduce-scatter.19
  960.9 21.3 reduce-scatter.15
  984.6 26.7 reduce-scatter.11
  1013.6 25.7 reduce-scatter.13
  1042.2 18.4 reduce-scatter.17
  1063.6 18.2 reduce-scatter.21
  1084.7 40.9 all-reduce.11
